TPU v7x, 32 devices: a whole 2x2x4 slice. The times are simulated.
32 devices in a mesh: shard: 2 (over x), ctx: 4 (over y, core), tp: 4 (over z).
Axes of the slice: x: 2, y: 2, z: 4, core: 2. Of those that a mesh axis runs over, the one named last changes fastest.
Arguments:
- tokens: bfloat16 [6, 608, 1024], P('shard', 'ctx'), may hold values from -6 to 6
- pad_mask: int32 [6, 608], P('shard', 'ctx'), may hold values from 0 to 1, as said below
- ln1_gain: float32 [1024], replicated, may hold values from 0.25 to 1.75
- ln1_shift: float32 [1024], replicated, may hold values from -3 to 3
- w_qkv: bfloat16 [3, 1024, 1024], P(None, 'shard', 'tp'), may hold values from -0.1875 to 0.1875
- b_qv: float32 [2, 1024], P(None, 'tp'), may hold values from -3 to 3
- w_out: bfloat16 [1024, 1024], P('tp', 'shard'), may hold values from -1 to 1
- b_out: float32 [1024], replicated, may hold values from -3 to 3
- ln2_gain: float32 [1024], replicated, may hold values from 0.25 to 1.75
- ln2_shift: float32 [1024], replicated, may hold values from -3 to 3
- w_up: bfloat16 [1024, 4096], P('shard', 'tp'), may hold values from -0.1875 to 0.1875
- b_up: float32 [4096], P('tp'), may hold values from -3 to 3
- w_down: bfloat16 [4096, 1024], P('tp', 'shard'), may hold values from -0.09375 to 0.09375
- b_down: float32 [1024], replicated, may hold values from -4 to 4
- cotangent: bfloat16 [6, 608, 1024], P('shard', 'ctx'), may hold values from -6 to 6
Outputs:
- out_tokens: float32 [6, 608, 1024], P('shard', 'ctx')
- grad_tokens: float32 [6, 608, 1024], P('shard', 'ctx')
- grad_w_qkv: float32 [3, 1024, 1024], P(None, 'shard', 'tp')
- grad_b_qv: float32 [2, 1024], P(None, 'tp')
- grad_w_out: float32 [1024, 1024], P('tp', 'shard')
- grad_b_out: float32 [1024], replicated
- grad_ln1_gain: float32 [1024], replicated
- grad_ln1_shift: float32 [1024], replicated
- grad_ln2_gain: float32 [1024], replicated
- grad_ln2_shift: float32 [1024], replicated
- grad_w_up: float32 [1024, 4096], P('shard', 'tp')
- grad_b_up: float32 [4096], P('tp')
- grad_w_down: float32 [4096, 1024], P('tp', 'shard')
- grad_b_down: float32 [1024], replicated
Inputs may be any that keep to these rules, and one draw needn't show every extreme that they name: `pad_mask`: each image has exactly 577 ones; the 31 padding slots may lie anywhere in the image.
All inputs are finite; a program needn't handle non-finite values.
Results may differ from a plain program's by a relative error of at most 0.02.
Values may be sent and summed in bfloat16 or wider, within the bound.
A program may use at most 128 MiB of HBM per device.

v0:
```python
import math

import jax
import jax.numpy as jnp
from jax import lax
from jax.sharding import PartitionSpec as P

HD = 64


NEG_FILL = -1e30


def normalize(values, gain, shift):
    row_mean = jnp.mean(values, axis=-1, keepdims=True)
    centred = values - row_mean
    inv_std = lax.rsqrt(jnp.mean(centred * centred, axis=-1, keepdims=True) + 1e-06)
    unit_rows = centred * inv_std
    return (unit_rows, inv_std, unit_rows * gain + shift)


def norm_back(upstream, unit_rows, inv_std, gain):
    scaled = upstream * gain
    centre = jnp.mean(scaled, axis=-1, keepdims=True)
    along = jnp.mean(scaled * unit_rows, axis=-1, keepdims=True)
    return inv_std * (scaled - centre - unit_rows * along)


def gelu_slope(pre_act):
    return (
        0.5 * (1.0 + lax.erf(pre_act * 0.7071067811865476))
        + pre_act * jnp.exp(-0.5 * pre_act * pre_act) * 0.3989422804014327
    )


def body(
    tokens,
    pad_mask,
    ln1_gain,
    ln1_shift,
    w_qkv,
    b_qv,
    w_out,
    b_out,
    ln2_gain,
    ln2_shift,
    w_up,
    b_up,
    w_down,
    b_down,
    cotangent,
):
    scale = 1.0 / math.sqrt(HD)
    images, piece, width = tokens.shape
    tok_count = images * piece
    qkv_full, out_full = (
        lax.all_gather(w_qkv, "shard", axis=1, tiled=True),
        lax.all_gather(w_out, "shard", axis=1, tiled=True),
    )
    up_full, down_full = (
        lax.all_gather(w_up, "shard", axis=0, tiled=True),
        lax.all_gather(w_down, "shard", axis=1, tiled=True),
    )
    local_width = out_full.shape[0]
    local_heads = local_width // HD
    inputs_wide = tokens.reshape(tok_count, width).astype(jnp.float32)
    first_unit, first_inv, first_norm = normalize(inputs_wide, ln1_gain, ln1_shift)
    first_low = first_norm.astype(jnp.bfloat16)
    projected = jnp.einsum("td,cdh->cth", first_low, qkv_full, preferred_element_type=jnp.float32)
    queries = (projected[0] + b_qv[0]).astype(jnp.bfloat16)
    key_local = projected[1].astype(jnp.bfloat16).reshape(images, piece, local_width)
    value_local = (projected[2] + b_qv[1]).astype(jnp.bfloat16).reshape(images, piece, local_width)
    valid_local = (pad_mask > 0).astype(jnp.bfloat16)
    key_all, value_all, valid_all = (
        lax.all_gather(key_local, "ctx", axis=1, tiled=True),
        lax.all_gather(value_local, "ctx", axis=1, tiled=True),
        lax.all_gather(valid_local, "ctx", axis=1, tiled=True),
    )
    seq_len = key_all.shape[1]
    query_heads = queries.reshape(images, piece, local_heads, HD)
    key_heads = key_all.reshape(images, seq_len, local_heads, HD)
    value_heads = value_all.reshape(images, seq_len, local_heads, HD)

    def masked_scores():
        scores = (
            jnp.einsum(
                "iqhe,ikhe->ihqk", query_heads, key_heads, preferred_element_type=jnp.float32
            )
            * scale
        )
        return jnp.where(valid_all[:, None, None, :] > 0.5, scores, NEG_FILL)

    scores = masked_scores()
    row_top = jnp.max(scores, axis=-1, keepdims=True)
    log_total = row_top + jnp.log(jnp.sum(jnp.exp(scores - row_top), axis=-1, keepdims=True))
    weights_low = jnp.exp(scores - log_total).astype(jnp.bfloat16)
    attended = jnp.einsum(
        "ihqk,ikhe->iqhe", weights_low, value_heads, preferred_element_type=jnp.float32
    )
    attended = attended.astype(jnp.bfloat16).reshape(tok_count, local_width)
    attn_part = jnp.dot(attended, out_full, preferred_element_type=jnp.float32)
    middle = (
        inputs_wide + lax.psum(attn_part.astype(jnp.bfloat16), "tp").astype(jnp.float32) + b_out
    )
    second_unit, second_inv, second_norm = normalize(middle, ln2_gain, ln2_shift)
    second_low = second_norm.astype(jnp.bfloat16)
    pre_act = jnp.dot(second_low, up_full, preferred_element_type=jnp.float32) + b_up
    activated = jax.nn.gelu(pre_act, approximate=False).astype(jnp.bfloat16)
    mlp_part = jnp.dot(activated, down_full, preferred_element_type=jnp.float32)
    result = middle + lax.psum(mlp_part.astype(jnp.bfloat16), "tp").astype(jnp.float32) + b_down
    out_tokens = result.reshape(images, piece, width)
    upstream_low = cotangent.reshape(tok_count, width)
    upstream_wide = upstream_low.astype(jnp.float32)
    act_grad = jnp.dot(upstream_low, down_full.T, preferred_element_type=jnp.float32) * gelu_slope(
        pre_act
    )
    act_low = act_grad.astype(jnp.bfloat16)
    grad_down = jnp.einsum("tf,td->fd", activated, upstream_low, preferred_element_type=jnp.float32)
    grad_up = jnp.einsum("td,tf->df", second_low, act_low, preferred_element_type=jnp.float32)
    norm2_part = jnp.dot(act_low, up_full.T, preferred_element_type=jnp.float32)
    norm2_grad = lax.psum(norm2_part.astype(jnp.bfloat16), "tp").astype(jnp.float32)
    middle_grad = upstream_wide + norm_back(norm2_grad, second_unit, second_inv, ln2_gain)
    middle_low = middle_grad.astype(jnp.bfloat16)
    grad_out = jnp.einsum("th,td->hd", attended, middle_low, preferred_element_type=jnp.float32)
    attended_grad = jnp.dot(middle_low, out_full.T, preferred_element_type=jnp.float32)
    attended_grad = attended_grad.astype(jnp.bfloat16).reshape(images, piece, local_heads, HD)
    weights = jnp.exp(masked_scores() - log_total)
    weights_low = weights.astype(jnp.bfloat16)
    weight_grad = jnp.einsum(
        "iqhe,ikhe->ihqk", attended_grad, value_heads, preferred_element_type=jnp.float32
    )
    row_dot = jnp.sum(weights * weight_grad, axis=-1, keepdims=True)
    score_grad = (scale * weights * (weight_grad - row_dot)).astype(jnp.bfloat16)
    query_grad = jnp.einsum(
        "ihqk,ikhe->iqhe", score_grad, key_heads, preferred_element_type=jnp.float32
    ).reshape(tok_count, local_width)
    key_part = jnp.einsum(
        "ihqk,iqhe->ikhe", score_grad, query_heads, preferred_element_type=jnp.float32
    ).reshape(images, seq_len, local_width)
    value_part = jnp.einsum(
        "ihqk,iqhe->ikhe", weights_low, attended_grad, preferred_element_type=jnp.float32
    ).reshape(images, seq_len, local_width)
    key_grad, value_grad = (
        lax.psum_scatter(
            key_part.astype(jnp.bfloat16), "ctx", scatter_dimension=1, tiled=True
        ).astype(jnp.float32),
        lax.psum_scatter(
            value_part.astype(jnp.bfloat16), "ctx", scatter_dimension=1, tiled=True
        ).astype(jnp.float32),
    )
    key_grad = key_grad.reshape(tok_count, local_width)
    value_grad = value_grad.reshape(tok_count, local_width)
    proj_grad = jnp.stack([query_grad, key_grad, value_grad]).astype(jnp.bfloat16)
    grad_qkv = jnp.einsum("td,cth->cdh", first_low, proj_grad, preferred_element_type=jnp.float32)
    norm1_part = jnp.einsum("cth,cdh->td", proj_grad, qkv_full, preferred_element_type=jnp.float32)
    norm1_grad = lax.psum(norm1_part.astype(jnp.bfloat16), "tp").astype(jnp.float32)
    input_grad = middle_grad + norm_back(norm1_grad, first_unit, first_inv, ln1_gain)
    grad_tokens = input_grad.reshape(images, piece, width)
    small = lax.psum(
        (
            jnp.stack([jnp.sum(query_grad, axis=0), jnp.sum(value_grad, axis=0)]),
            jnp.sum(middle_grad, axis=0),
            jnp.sum(norm1_grad * first_unit, axis=0),
            jnp.sum(norm1_grad, axis=0),
            jnp.sum(norm2_grad * second_unit, axis=0),
            jnp.sum(norm2_grad, axis=0),
            jnp.sum(act_grad, axis=0),
            jnp.sum(upstream_wide, axis=0),
        ),
        ("shard", "ctx"),
    )
    summed = (
        lax.psum(grad_qkv.astype(jnp.bfloat16), "ctx").astype(jnp.float32),
        lax.psum(grad_out.astype(jnp.bfloat16), "ctx").astype(jnp.float32),
        lax.psum(grad_up.astype(jnp.bfloat16), "ctx").astype(jnp.float32),
        lax.psum(grad_down.astype(jnp.bfloat16), "ctx").astype(jnp.float32),
    )
    big_sums = (
        lax.psum_scatter(
            summed[0].astype(jnp.bfloat16), "shard", scatter_dimension=1, tiled=True
        ).astype(jnp.float32),
        lax.psum_scatter(
            summed[1].astype(jnp.bfloat16), "shard", scatter_dimension=1, tiled=True
        ).astype(jnp.float32),
        lax.psum_scatter(
            summed[2].astype(jnp.bfloat16), "shard", scatter_dimension=0, tiled=True
        ).astype(jnp.float32),
        lax.psum_scatter(
            summed[3].astype(jnp.bfloat16), "shard", scatter_dimension=1, tiled=True
        ).astype(jnp.float32),
    )
    return (
        out_tokens,
        grad_tokens,
        big_sums[0],
        small[0],
        big_sums[1],
        small[1],
        small[2],
        small[3],
        small[4],
        small[5],
        big_sums[2],
        small[6],
        big_sums[3],
        small[7],
    )


def solution(mesh):
    return jax.shard_map(
        body,
        mesh=mesh,
        in_specs=(
            P("shard", "ctx", None),
            P("shard", "ctx"),
            P(),
            P(),
            P(None, "shard", "tp"),
            P(None, "tp"),
            P("tp", "shard"),
            P(),
            P(),
            P(),
            P("shard", "tp"),
            P("tp"),
            P("tp", "shard"),
            P(),
            P("shard", "ctx", None),
        ),
        out_specs=(
            P("shard", "ctx", None),
            P("shard", "ctx", None),
            P(None, "shard", "tp"),
            P(None, "tp"),
            P("tp", "shard"),
            P(),
            P(),
            P(),
            P(),
            P(),
            P("shard", "tp"),
            P("tp"),
            P("tp", "shard"),
            P(),
        ),
        check_vma=False,
    )
```

profile of v0, /device:TPU:0, one launch (start us, length us, event | category | flops | bytes accessed | tf_op | source)
XLA Modules:
  0.0 626.5 jit_solution(8793724352426675898)
XLA Ops:
  8.0 0.8 slice_reduce_fusion
  8.8 1.4 convert_reduce_fusion.2
  10.9 6.2 all-gather
  17.2 14.5 %all_gather.25 = bf16[256,1024]{1,0:T(8,128)(2,1)S(1)} all-gather(bf16[256,512]{1,0:T(8,128)(2,1)S(1)} %copy-done.19), channel_id=1, replica_groups=mesh['shard'=2,'ctx'=4,'tp'=4] {'shard'}, dimensions={1}, use_global_device_ids=true | all-gather | bytes 786432 | tf_op jit(solution)/shard_map/all_gather | solution.py:58
  31.7 1.7 bitcast_subtract_fusion
  33.4 10.4 %all-gather.5.cloned.1.call-done = bf16[3,1024,256]{2,1,0:T(8,128)(2,1)} async-done(((bf16[3,512,256]{2,1,0:T(8,128)(2,1)}), bf16[3,1024,256]{2,1,0:T(8,128)(2,1)}) %all-gather.5.cloned.1.call-update) | async-done | bytes 1572880 | tf_op jit(solution)/shard_map/all_gather | solution.py:57
  43.7 2.3 convolution_bitcast_fusion
  46.8 0.8 fusion.55
  47.6 1.4 squeeze.8
  49.0 0.9 add_convert_fusion.2
  50.0 1.3 copy.66
  51.3 11.4 %all_gather.24 = bf16[3,608,256]{2,1,0:T(8,128)(2,1)} all-gather(bf16[3,152,256]{2,1,0:T(8,128)(2,1)} %bitcast.92), channel_id=1, replica_groups=mesh['shard'=2,'ctx'=4,'tp'=4] {'ctx'}, dimensions={1}, use_global_device_ids=true | all-gather | bytes 1167360 | tf_op jit(solution)/shard_map/all_gather | solution.py:75
  62.7 1.5 copy.65
  64.3 10.0 %all_gather.22 = bf16[3,608,256]{2,1,0:T(8,128)(2,1)} all-gather(bf16[3,152,256]{2,1,0:T(8,128)(2,1)S(1)} %add_convert_fusion.3), channel_id=1, replica_groups=mesh['shard'=2,'ctx'=4,'tp'=4] {'ctx'}, dimensions={1}, use_global_device_ids=true | all-gather | bytes 1167360 | tf_op jit(solution)/shard_map/all_gather | solution.py:76
  74.2 2.2 copy.63
  76.5 1.1 fusion
  77.6 1.5 exponential_reduce_fusion
  79.7 1.3 fusion.36
  81.6 1.3 convolution_convert_fusion.7
  84.5 47.4 %all-reduce.12.cloned.1.call-done = bf16[456,1024]{1,0:T(8,128)(2,1)} async-done(((bf16[456,1024]{1,0:T(8,128)(2,1)}), bf16[456,1024]{1,0:T(8,128)(2,1)}) %all-reduce.12.cloned.1.call-update) | async-done | bytes 933904 | tf_op jit(solution)/shard_map/psum | solution.py:103
  131.9 1.5 bitcast_add_fusion
  135.1 30.7 %all-gather.7.cloned.1.call-done = bf16[1024,1024]{1,0:T(8,128)(2,1)} async-done(((bf16[512,1024]{1,0:T(8,128)(2,1)}), bf16[1024,1024]{1,0:T(8,128)(2,1)}) %all-gather.7.cloned.1.call-update) | async-done | bytes 2097168 | tf_op jit(solution)/shard_map/all_gather | solution.py:61
  165.8 7.8 %fusion.18 = (bf16[456,1024]{1,0:T(8,128)(2,1)}, f32[456,1024]{1,0:T(8,128)}) fusion(f32[1024]{0:T(1024)S(1)} %copy-done.28, bf16[1024,1024]{1,0:T(8,128)(2,1)} %all-gather.7.cloned.1.call-done, f32[456,1024]{1,0:T(8,128)S(1)} %subtract_multiply_fusion, f32[1024]{0:T(1024)S(1)} %copy-done.29, f32[1024]{0:T(1024)S(1)} %copy-done.22), kind=kOutput, calls=%fused_computation.33 | convolution fusion | flops 988520448 | bytes 6778880 | tf_op jit(solution)/shard_map/dot_general | solution.py:107
  173.6 26.7 %all-gather.9.cloned.1.call-done = bf16[1024,1024]{1,0:T(8,128)(2,1)} async-done(((bf16[1024,512]{1,0:T(8,128)(2,1)}), bf16[1024,1024]{1,0:T(8,128)(2,1)}) %all-gather.9.cloned.1.call-update) | async-done | bytes 2097168 | tf_op jit(solution)/shard_map/all_gather | solution.py:62
  200.3 4.3 fusion.57
  204.6 0.9 copy-done.31
  205.5 2.1 convolution_convert_fusion.5
  207.7 48.7 %all-reduce.14.cloned.1.call-done = bf16[456,1024]{1,0:T(8,128)(2,1)} async-done(((bf16[456,1024]{1,0:T(8,128)(2,1)}), bf16[456,1024]{1,0:T(8,128)(2,1)}) %all-reduce.14.cloned.1.call-update) | async-done | bytes 933904 | tf_op jit(solution)/shard_map/psum | solution.py:121
  256.4 2.0 fusion.24
  258.5 2.1 fusion.53
  260.6 1.1 convolution_convert_fusion.10
  261.7 1.2 reshape.161
  262.9 1.1 copy.68
  264.0 4.8 convolution_convert_fusion.3
  268.8 5.0 multiply_reduce_fusion
  273.8 3.3 copy.74
  277.1 4.5 multiply_convert_fusion
  281.7 1.7 convolution_convert_fusion.4
  283.4 3.4 copy.71
  287.1 1.3 convolution_convert_fusion.8
  288.4 4.4 convolution_convert_fusion.1
  292.9 4.1 convolution_convert_fusion
  298.8 3.8 fusion.56
  302.6 1.3 copy.69
  304.3 39.7 %all-reduce.20.cloned.1.call-done = (bf16[3,608,256]{2,0,1:T(4,128)(2,1)}, bf16[3,608,256]{2,0,1:T(4,128)(2,1)}) async-done(((bf16[3,608,256]{2,0,1:T(4,128)(2,1)}, bf16[3,608,256]{2,0,1:T(4,128)(2,1)}), (bf16[3,608,256]{2,0,1:T(4,128)(2,1)}, bf16[3,608,256]{2,0,1:T(4,128)(2,1)})) %all-reduce.20.cloned.1.call-update) | async-done | bytes 1867792
  343.9 1.2 constant_dynamic-slice_fusion.1
  345.1 1.3 convert_reduce_fusion.4
  346.4 2.2 fusion.35
  348.7 4.1 convolution_convert_fusion.6
  352.8 1.9 bitcast_convert_fusion
  354.7 6.7 %reduce-scatter.7.cloned.1.call-done = bf16[256,512]{1,0:T(8,128)(2,1)} async-done(((bf16[256,1024]{1,0:T(8,128)(2,1)}), bf16[256,512]{1,0:T(8,128)(2,1)}) %reduce-scatter.7.cloned.1.call-update) | async-done | bytes 262160 | tf_op jit(solution)/shard_map/reduce_scatter | solution.py:182
  361.5 34.8 %reduce-scatter.9.cloned.1.call-done = bf16[512,1024]{1,0:T(8,128)(2,1)} async-done(((bf16[1024,1024]{1,0:T(8,128)(2,1)}), bf16[512,1024]{1,0:T(8,128)(2,1)}) %reduce-scatter.9.cloned.1.call-update) | async-done | bytes 1048592 | tf_op jit(solution)/shard_map/reduce_scatter | solution.py:185
  396.2 34.8 %reduce-scatter.11.cloned.1.call-done = bf16[1024,512]{1,0:T(8,128)(2,1)} async-done(((bf16[1024,1024]{1,0:T(8,128)(2,1)}), bf16[1024,512]{1,0:T(8,128)(2,1)}) %reduce-scatter.11.cloned.1.call-update) | async-done | bytes 1048592 | tf_op jit(solution)/shard_map/reduce_scatter | solution.py:188
  431.0 28.8 %reduce-scatter.5.cloned.1.call-done = bf16[3,512,256]{1,2,0:T(8,128)(2,1)} async-done(((bf16[3,1024,256]{1,2,0:T(8,128)(2,1)}), bf16[3,512,256]{1,2,0:T(8,128)(2,1)}) %reduce-scatter.5.cloned.1.call-update) | async-done | bytes 786448 | tf_op jit(solution)/shard_map/reduce_scatter | solution.py:179
  459.8 1.4 convert_reduce_fusion.3
  461.3 80.3 %all-reduce.16.cloned.1.call-done = (bf16[456,1024]{1,0:T(8,128)(2,1)}, bf16[456,1024]{1,0:T(8,128)(2,1)}) async-done(((bf16[456,1024]{1,0:T(8,128)(2,1)}, bf16[456,1024]{1,0:T(8,128)(2,1)}), (bf16[456,1024]{1,0:T(8,128)(2,1)}, bf16[456,1024]{1,0:T(8,128)(2,1)})) %all-reduce.16.cloned.1.call-update) | async-done | bytes 1867792 | tf_op jit(solution)/shard_map/psum | solution.py:110
  541.6 2.8 fusion.6
  544.4 24.2 %all-reduce.2 = (f32[2,256]{1,0:T(2,128)}, f32[1024]{0:T(1024)}, f32[1024]{0:T(1024)}, f32[1024]{0:T(1024)}, f32[1024]{0:T(1024)}, /*index=5*/f32[1024]{0:T(1024)}, f32[1024]{0:T(1024)}, f32[1024]{0:T(1024)}) all-reduce(f32[2,256]{1,0:T(2,128)S(1)} %pad_maximum_fusion.3, ...), channel_id=1, replica_groups=mesh['shard'=2,'ctx'=4,'tp'=4] {'shard','ctx'}, use_global_device_ids=true, to_apply=%region_21.22 | all-reduce | flops 7680 | bytes 61440 | tf_op jit(solution)/shard_map/psum | solution.py:159
  568.6 4.5 fusion.10
  573.1 38.9 %all-reduce.18.cloned.1.call-done = (bf16[3,512,256]{1,2,0:T(8,128)(2,1)}, bf16[256,512]{1,0:T(8,128)(2,1)}, bf16[512,1024]{1,0:T(8,128)(2,1)}, bf16[1024,512]{1,0:T(8,128)(2,1)}) async-done(((bf16[3,512,256]{1,2,0:T(8,128)(2,1)}, bf16[256,512]{1,0:T(8,128)(2,1)}, bf16[512,1024]{1,0:T(8,128)(2,1)}, bf16[1024,512]{1,0:T(8,128)(2,1)}), (bf16[3,512,256]{1,2,0:T(8,128)(2,1)}, bf16[256,512]{1,0:T(8,128)(2,1)}, ...) | async-done | bytes 3145744 | tf_op jit(solution)/shard_map/psum | solution.py:173
  612.0 1.9 convert_element_type.182
  613.9 2.5 copy.76
  616.5 1.6 convert_element_type.184
  618.0 1.6 convert_element_type.186
  (115 shorter events, 9.0 us)
Async XLA Ops:
  7.2 3.2 copy-start.1
  7.2 3.7 copy-start.24
  7.2 10.0 %copy-start.19 = (bf16[256,512]{1,0:T(8,128)(2,1)S(1)}, bf16[256,512]{1,0:T(8,128)(2,1)}, u32[]{:S(2)}) copy-start(bf16[256,512]{1,0:T(8,128)(2,1)} %param.21) | copy-start | bytes 786436
  7.2 24.5 %copy-start.21 = (f32[1024]{0:T(1024)S(1)}, f32[1024]{0:T(1024)}, u32[]{:S(2)}) copy-start(f32[1024]{0:T(1024)} %param.17) | copy-start | bytes 12292
  7.2 24.5 %copy-start.25 = (f32[1024]{0:T(1024)S(1)}, f32[1024]{0:T(1024)}, u32[]{:S(2)}) copy-start(f32[1024]{0:T(1024)} %param.18) | copy-start | bytes 12292
  7.2 36.5 %all-gather.5.cloned.1.call-start = ((), (), s32[]{:S(2)}) async-start(), calls=%async_computation.4 | async-start | bytes 2359296 | tf_op jit(solution)/shard_map/all_gather | solution.py:57
  8.0 124.0 %all-reduce.12.cloned.1.call-start = ((), (), s32[]{:S(2)}) async-start(), calls=%async_computation.5 | async-start | bytes 1867776 | tf_op jit(solution)/shard_map/psum | solution.py:103
  33.3 12.7 %copy-start.17 = (bf16[456,1024]{1,0:T(8,128)(2,1)}, bf16[456,1024]{1,0:T(8,128)(2,1)S(1)}, u32[]{:S(2)}) copy-start(bf16[456,1024]{1,0:T(8,128)(2,1)S(1)} %get-tuple-element.101) | copy-start | bytes 2801668
  51.2 25.2 %copy-start.6 = (bf16[3,152,4,64]{1,3,2,0:T(8,128)(2,1)}, bf16[3,152,4,64]{1,3,2,0:T(8,128)(2,1)S(1)}, u32[]{:S(2)}) copy-start(bf16[3,152,4,64]{1,3,2,0:T(8,128)(2,1)S(1)} %copy.66) | copy-start | bytes 700420
  64.2 12.2 %copy-start.4 = (bf16[3,608,256]{1,2,0:T(8,128)(2,1)}, bf16[3,608,256]{1,2,0:T(8,128)(2,1)S(1)}, u32[]{:S(2)}) copy-start(bf16[3,608,256]{1,2,0:T(8,128)(2,1)S(1)} %copy.65) | copy-start | bytes 2801668
  77.6 2.1 copy-start
  77.6 2.1 copy-start.8
  81.6 2.7 copy-start.12
  83.0 82.8 %all-gather.7.cloned.1.call-start = ((), (), s32[]{:S(2)}) async-start(), calls=%async_computation.6 | async-start | bytes 3145728 | tf_op jit(solution)/shard_map/all_gather | solution.py:61
  83.7 116.6 %all-gather.9.cloned.1.call-start = ((), (), s32[]{:S(2)}) async-start(), calls=%async_computation.7 | async-start | bytes 3145728 | tf_op jit(solution)/shard_map/all_gather | solution.py:62
  84.3 49.2 %copy-start.20 = (f32[1024]{0:T(1024)S(1)}, f32[1024]{0:T(1024)}, u32[]{:S(2)}) copy-start(f32[1024]{0:T(1024)} %param.22) | copy-start | bytes 12292
  84.3 172.1 %all-reduce.14.cloned.1.call-start = ((), (), s32[]{:S(2)}) async-start(), calls=%async_computation.8 | async-start | bytes 1867776 | tf_op jit(solution)/shard_map/psum | solution.py:121
  133.5 1.2 copy-start.5
  134.7 31.1 %copy-start.22 = (f32[1024]{0:T(1024)S(1)}, f32[1024]{0:T(1024)}, u32[]{:S(2)}) copy-start(f32[1024]{0:T(1024)} %param.23) | copy-start | bytes 12292
  134.7 31.1 %copy-start.28 = (f32[1024]{0:T(1024)S(1)}, f32[1024]{0:T(1024)}, u32[]{:S(2)}) copy-start(f32[1024]{0:T(1024)} %param.26) | copy-start | bytes 12292
  134.7 31.1 %copy-start.29 = (f32[1024]{0:T(1024)S(1)}, f32[1024]{0:T(1024)}, u32[]{:S(2)}) copy-start(f32[1024]{0:T(1024)} %param.24) | copy-start | bytes 12292
  135.1 121.4 %copy-start.3 = (f32[456,1024]{1,0:T(8,128)}, f32[456,1024]{1,0:T(8,128)S(1)}, u32[]{:S(2)}) copy-start(f32[456,1024]{1,0:T(8,128)S(1)} %subtract_multiply_fusion) | copy-start | bytes 5603332
  200.3 5.2 copy-start.26
  204.6 0.9 copy-start.31
  207.6 136.3 %all-reduce.20.cloned.1.call-start = ((), (), s32[]{:S(2)}) async-start(), calls=%async_computation.15 | async-start | bytes 4980736
  256.4 2.0 copy-start.10
  256.4 2.0 copy-start.11
  264.0 4.8 copy-start.9
  264.0 4.8 copy-start.14
  277.1 4.5 copy-start.7
  281.7 1.7 copy-start.2
  283.4 3.7 copy-start.13
  286.8 74.7 %reduce-scatter.7.cloned.1.call-start = ((), (), s32[]{:S(2)}) async-start(), calls=%async_computation.10 | async-start | bytes 786432 | tf_op jit(solution)/shard_map/reduce_scatter | solution.py:182
  288.4 107.9 %reduce-scatter.9.cloned.1.call-start = ((), (), s32[]{:S(2)}) async-start(), calls=%async_computation.11 | async-start | bytes 3145728 | tf_op jit(solution)/shard_map/reduce_scatter | solution.py:185
  292.8 138.2 %reduce-scatter.11.cloned.1.call-start = ((), (), s32[]{:S(2)}) async-start(), calls=%async_computation.12 | async-start | bytes 3145728 | tf_op jit(solution)/shard_map/reduce_scatter | solution.py:188
  297.0 0.7 copy-start.30
  297.0 162.8 %reduce-scatter.5.cloned.1.call-start = ((), (), s32[]{:S(2)}) async-start(), calls=%async_computation.9 | async-start | bytes 2359296 | tf_op jit(solution)/shard_map/reduce_scatter | solution.py:179
  343.9 2.5 copy-start.18
  348.7 192.9 %all-reduce.16.cloned.1.call-start = ((), (), s32[]{:S(2)}) async-start(), calls=%async_computation.13 | async-start | bytes 3735552 | tf_op jit(solution)/shard_map/psum | solution.py:110
  348.7 4.1 copy-start.27
  354.7 257.3 %all-reduce.18.cloned.1.call-start = ((), (), s32[]{:S(2)}) async-start(), calls=%async_computation.14 | async-start | bytes 6291456 | tf_op jit(solution)/shard_map/psum | solution.py:173
  541.6 27.0 %copy-start.23 = (f32[1024]{0:T(1024)S(1)}, f32[1024]{0:T(1024)}, u32[]{:S(2)}) copy-start(f32[1024]{0:T(1024)} %param.28) | copy-start | bytes 12292
  612.0 4.4 copy-start.16
  616.5 1.6 copy-start.15
Sparse Core Ops, SparseCore 0:
  9.6 34.1 all-gather.4
  83.1 48.8 all-reduce.11
  133.5 32.2 all-gather.6
  167.2 33.0 all-gather.8
  207.8 48.6 all-reduce.13
  286.9 56.9 all-reduce.19
  346.7 14.6 reduce-scatter.6
  364.3 31.8 reduce-scatter.8
  399.0 31.8 reduce-scatter.10
  433.6 26.1 reduce-scatter.4
  462.8 78.6 all-reduce.15
  544.0 67.9 all-reduce.17
where the time goes:
time: 628 us; the launch traced here: 627 us
  waiting for transfers between devices  430 us (68%)
  blocking collectives  66.3 us (11%)
  matrix products  54.6 us (9%)
  other arithmetic  32.1 us (5%)
  local copies, waits for them, and re-layouts  27.5 us (4%)
  between operations  15.3 us (2%)
    psum x1, waiting for transfers between devices, body(): lax.psum(mlp_part.astype(jnp.bfloat16), 'tp').astype(jnp.float32)  80.3 us
    psum x1, waiting for transfers between devices, body(): lax.psum(norm2_part.astype(jnp.bfloat16), 'tp').astype(jnp.float32)  48.7 us
    psum x1, waiting for transfers between devices, body(): lax.psum(attn_part.astype(jnp.bfloat16), 'tp').astype(jnp.float32)  47.4 us
    unnamed x13, waiting for transfers between devices  41.7 us
    psum x1, waiting for transfers between devices, body(): lax.psum(grad_qkv.astype(jnp.bfloat16), 'ctx').astype(jnp.float32)  38.9 us
    reduce_scatter x1, waiting for transfers between devices, body(): lax.psum_scatter(summed[3].astype(jnp.bfloat16), 'shard', scatter_dimensi...  34.8 us
    reduce_scatter x1, waiting for transfers between devices, body(): lax.psum_scatter(summed[2].astype(jnp.bfloat16), 'shard', scatter_dimensi...  34.8 us
    all_gather x1, waiting for transfers between devices, body(): lax.all_gather(w_up, 'shard', axis=0, tiled=True)  30.7 us
  transfers between devices with their start and end apart: 12, of which 12 were waited for; matrix products, arithmetic and copies ran while one was open for 8% of the time, Pallas kernels for 0%

commit v1 on v0

v1 whole, which is shorter than its diff:
```python
import functools
import math
import types

import jax
import jax.numpy as jnp
from jax import lax
from jax.experimental import pallas as pl
from jax.experimental.pallas import tpu as pltpu
from jax.sharding import PartitionSpec as P

HD = 64
BIG = 1e30
MESH = pl.DeviceIdType.MESH
BF, F32 = jnp.bfloat16, jnp.float32
RB = 32
TILE = 256


def dot(a, b):
    return lax.dot_general(a, b, (((1,), (0,)), ((), ())), preferred_element_type=F32)


def dot_nt(a, b):
    return lax.dot_general(a, b, (((1,), (1,)), ((), ())), preferred_element_type=F32)


def dot_tn(a, b):
    return lax.dot_general(a, b, (((0,), (0,)), ((), ())), preferred_element_type=F32)


def norm_stats(x):
    centred = x - jnp.mean(x, axis=-1, keepdims=True)
    inv = lax.rsqrt(jnp.mean(centred * centred, axis=-1, keepdims=True) + 1e-06)
    return centred * inv, inv


def norm_back(upstream, unit, inv, gain):
    scaled = upstream * gain
    centre = jnp.mean(scaled, axis=-1, keepdims=True)
    along = jnp.mean(scaled * unit, axis=-1, keepdims=True)
    return inv * (scaled - centre - unit * along)


def fold8(x):
    return jnp.sum(x.reshape(x.shape[0] // 8, 8, x.shape[1]), axis=0)


def aligned(i, m):
    return pl.multiple_of(i, m)


class Dims:
    pass


def dims_of(mesh, tokens, w_out, w_up):
    d = Dims()
    d.S, d.C, d.T = (mesh.shape[a] for a in ("shard", "ctx", "tp"))
    assert d.C == 4 and d.T == 4
    d.images, d.piece, d.width = tokens
    d.rows = -(-d.piece // RB) * RB
    d.part = d.width // d.S
    d.local = w_out[0]
    d.hidden = w_up[1]
    d.heads = d.local // HD
    d.keys = d.C * d.rows
    return d


KV, Q, OUT, UP, DN, QKV = range(6)


def scratch_of(d):
    I, R, D, W, F, S, C = d.images, d.rows, d.width, d.local, d.hidden, d.S, d.C
    bf = lambda *shape: pltpu.VMEM(shape, BF)
    f32 = lambda *shape: pltpu.VMEM(shape, F32)
    scratch = dict(
        tok=bf(I, R, D),
        cot=bf(I, R, D),
        maskw=f32(8, TILE),
        first=bf(I, R, D),
        wqkv=bf(3, D, W),
        wout=bf(W, D),
        wup=bf(D, F),
        wdn=bf(F, D),
        q=bf(I, R, W),
        kv=bf(C, I, 2, R, W),
        wts=bf(I, d.heads * R, d.keys),
        att=bf(I, R, W),
        middle=f32(I, R, D),
        second=bf(I, R, D),
        activ=bf(I, R, F),
        actlow=bf(I, R, F),
        mgrad=f32(I, R, D),
        mlow=bf(I, R, D),
        dss=bf(d.heads * R, d.keys),
        qst=bf(d.heads * R, W),
        ost=bf(d.heads * R, W),
        dkv=bf(C, I, 2, R, W),
        rxa=bf(2, I, 2, R, W),
        rxb=bf(I, 2, R, W),
        pg=bf(3, I, R, W),
        acc=f32(8, 8, D),
        sm=f32(8, D),
        smx=f32(S * C, 8, D),
        gqkv=bf(3, D, W),
        gout=bf(W, D),
        gup=bf(D, F),
        gdn=bf(F, D),
        r1qkv=bf(3, D, W // 2),
        r1out=bf(W // 2, D),
        r1up=bf(D, F // 2),
        r1dn=bf(F // 2, D),
        r2qkv=bf(S, 3, D // S, W // 2),
        r2out=bf(S, W // 2, D // S),
        r2up=bf(S, D // S, F // 2),
        r2dn=bf(S, F // 2, D // S),
        r3qkv=bf(3, D // S, W // 2),
        r3out=bf(W // 2, D // S),
        r3up=bf(D // S, F // 2),
        r3dn=bf(F // 2, D // S),
    )
    full = lambda: bf(I, R, D)
    scratch.update(own1=full(), own2=full(), own3=full(), own4=full())
    scratch.update(tot1=full(), tot2=full(), tot3=full(), tot4=full())
    scratch.update(in01=full(), in02=full(), in03=full())
    scratch.update(in11=full(), in12=full(), in13=full())
    scratch["ssem"] = pltpu.SemaphoreType.DMA((MAX_COPIES * S // 2,))
    scratch["rsem"] = pltpu.SemaphoreType.DMA((MAX_COPIES * S // 2,))
    scratch["lsem"] = pltpu.SemaphoreType.DMA((64,))
    return scratch


MAX_COPIES = 200


class Net:
    def __init__(self, ssem, rsem, lsem):
        self.ssem, self.rsem, self.lsem = ssem, rsem, lsem
        self.n = self.m = 0
        self.sent = []
        self.stored = []

    def remote(self, src, dst, device):
        i, self.n = self.n, self.n + 1
        return pltpu.make_async_remote_copy(
            src_ref=src,
            dst_ref=dst,
            send_sem=self.ssem.at[i],
            recv_sem=self.rsem.at[i],
            device_id=device,
            device_id_type=MESH,
        )

    def local(self, src, dst):
        i, self.m = self.m, self.m + 1
        return pltpu.make_async_copy(src, dst, self.lsem.at[i])


def body_kernel(d, names, *refs):
    r = types.SimpleNamespace(**dict(zip(names, refs)))
    I, R, D, W, F, S, C = d.images, d.rows, d.width, d.local, d.hidden, d.S, d.C
    piece, part, heads, keys = d.piece, d.part, d.heads, d.keys
    s, c, t = lax.axis_index("shard"), lax.axis_index("ctx"), lax.axis_index("tp")
    core = lax.rem(c, 2)
    mate = c + 1 - 2 * core
    across = lax.rem(c + 2, 4)
    far = lax.rem(mate + 2, 4)
    tmate = t + 1 - 2 * lax.rem(t, 2)
    tpeer = 3 - t
    inner = lax.rem(t + 1, 4) >= 2
    edge = lax.rem(t + 1, 4) < 2
    on_mate, on_across = (s, mate, t), (s, across, t)
    net = Net(r.ssem, r.rsem, r.lsem)
    sent = net.sent

    def go(copy):
        copy.start()
        sent.append((None, copy))

    loads = {}
    for i in range(I):
        loads["tok", i] = net.local(r.tok_h.at[i], r.tok.at[i, pl.ds(0, piece)])
    rows_s = pl.ds(aligned(s * part, part), part)
    loads[KV] = net.local(r.wqkv_h.at[pl.ds(1, 2)], r.wqkv.at[pl.ds(1, 2), rows_s])
    loads[Q] = net.local(r.wqkv_h.at[pl.ds(0, 1)], r.wqkv.at[pl.ds(0, 1), rows_s])
    loads[OUT] = net.local(r.wout_h, r.wout.at[:, rows_s])
    loads[UP] = net.local(r.wup_h, r.wup.at[rows_s])
    loads[DN] = net.local(r.wdn_h, r.wdn.at[:, rows_s])
    for i in range(I):
        loads["cot", i] = net.local(r.cot_h.at[i], r.cot.at[i, pl.ds(0, piece)])
    for copy in loads.values():
        copy.start()

    barrier = pltpu.get_barrier_semaphore()
    for ds in range(S):
        for dc in range(C):
            if ds or dc:
                where = (lax.rem(s + ds, S), lax.rem(c + dc, C), t)
                pl.semaphore_signal(barrier, inc=1, device_id=where, device_id_type=MESH)
    pl.semaphore_signal(barrier, inc=1, device_id=(s, c, tmate), device_id_type=MESH)

    @pl.when(inner)
    def _():
        pl.semaphore_signal(barrier, inc=1, device_id=(s, c, tpeer), device_id_type=MESH)
        pl.semaphore_wait(barrier, S * C + 1)

    @pl.when(edge)
    def _():
        pl.semaphore_wait(barrier, S * C)

    def half_of(name, ref, shard, half):
        rows = pl.ds(aligned(shard * part, part), part)
        if name in (KV, Q):
            planes = pl.ds(1, 2) if name == KV else pl.ds(0, 1)
            return ref.at[planes, rows, pl.ds(aligned(half * (W // 2), W // 2), W // 2)]
        if name == OUT:
            return ref.at[pl.ds(aligned(half * (W // 2), W // 2), W // 2), rows]
        if name == UP:
            return ref.at[rows, pl.ds(aligned(half * (F // 2), F // 2), F // 2)]
        return ref.at[pl.ds(aligned(half * (F // 2), F // 2), F // 2), rows]

    def own_half(name, ref, half):
        if name in (KV, Q):
            planes = pl.ds(1, 2) if name == KV else pl.ds(0, 1)
            return ref.at[planes, :, pl.ds(aligned(half * (W // 2), W // 2), W // 2)]
        if name == OUT:
            return ref.at[pl.ds(aligned(half * (W // 2), W // 2), W // 2), :]
        if name == UP:
            return ref.at[:, pl.ds(aligned(half * (F // 2), F // 2), F // 2)]
        return ref.at[pl.ds(aligned(half * (F // 2), F // 2), F // 2), :]

    weights = {
        KV: (r.wqkv_h, r.wqkv),
        Q: (r.wqkv_h, r.wqkv),
        OUT: (r.wout_h, r.wout),
        UP: (r.wup_h, r.wup),
        DN: (r.wdn_h, r.wdn),
    }
    gather, spread = {}, {}
    for name, (source, full) in weights.items():
        for ds in range(1, S):
            to = (lax.rem(s + ds, S), c, t)
            copy = net.remote(
                own_half(name, source, core), half_of(name, full, s, core), to
            )
            go(copy)
            gather[name, ds] = copy
            owner = lax.rem(s + S - ds, S)
            held = half_of(name, full, owner, core)
            spread[name, ds] = net.remote(held, held, on_mate)

    def pass_on(name):
        for ds in range(1, S):
            gather[name, ds].wait_recv()
            go(spread[name, ds])

    def weight_ready(name):
        loads[name].wait()
        for ds in range(1, S):
            spread[name, ds].wait_recv()

    tail = piece // 16 * 16

    def clear_tail(ref, i):
        if tail < R:
            old = ref[i, pl.ds(tail, R - tail), :].astype(F32)
            row = lax.broadcasted_iota(jnp.int32, old.shape, 0)
            ref[i, pl.ds(tail, R - tail), :] = jnp.where(row < piece - tail, old, 0.0).astype(BF)

    def blocks(fn):
        def step(b, _):
            fn(pl.ds(aligned(b * RB, RB), RB))
            return 0

        lax.fori_loop(0, R // RB, step, 0)

    def tiles(n, fn):
        def step(b, _):
            fn(pl.ds(aligned(b * TILE, TILE), TILE))
            return 0

        lax.fori_loop(0, n // TILE, step, 0)

    r.acc[...] = jnp.zeros_like(r.acc)
    r.sm[...] = jnp.zeros_like(r.sm)
    r.maskw[...] = jnp.zeros_like(r.maskw)
    r.maskw[0:I, 0:piece] = (r.mask[...] > 0).astype(F32)

    def first_norm(i):
        loads["tok", i].wait()
        clear_tail(r.tok, i)

        def rows(w):
            unit, _ = norm_stats(r.tok[i, w, :].astype(F32))
            r.first[i, w, :] = (unit * r.g1[...] + r.b1[...]).astype(BF)

        blocks(rows)

    for i in range(I):
        first_norm(i)
    pass_on(KV)
    weight_ready(KV)

    kv_mate, kv_across, kv_far = {}, {}, {}
    row_w = lax.broadcasted_iota(jnp.int32, (R, W), 0)

    def keys_values(i):
        x = r.first[i]
        key = dot(x, r.wqkv[1])
        flags = jnp.broadcast_to(r.maskw[i : i + 1, :], (R, W))
        r.kv[c, i, 0] = jnp.where(row_w == piece, flags, key).astype(BF)
        r.kv[c, i, 1] = (dot(x, r.wqkv[2]) + r.bqv[1:2, :]).astype(BF)
        mine = r.kv.at[c, i]
        kv_across[i] = net.remote(mine, mine, on_across)
        kv_mate[i] = net.remote(mine, mine, on_mate)
        theirs = r.kv.at[across, i]
        kv_far[i] = net.remote(theirs, theirs, on_mate)
        go(kv_across[i])
        go(kv_mate[i])

    for i in range(I):
        keys_values(i)
    pass_on(Q)
    weight_ready(Q)
    for i in range(I):
        r.q[i] = (dot(r.first[i], r.wqkv[0]) + r.bqv[0:1, :]).astype(BF)
    pass_on(OUT)

    lane_head = lax.broadcasted_iota(jnp.int32, (R, W), 1) // HD
    scale = 1.0 / math.sqrt(HD)

    def all_keys(i):
        k = jnp.concatenate([r.kv[b, i, 0] for b in range(C)], axis=0)
        v = jnp.concatenate([r.kv[b, i, 1] for b in range(C)], axis=0)
        return k, v

    def key_bias(i):
        row = lax.broadcasted_iota(jnp.int32, (R, W), 0)
        lane = lax.broadcasted_iota(jnp.int32, (R, W), 1)
        lane1 = lax.broadcasted_iota(jnp.int32, (R, 128), 1)
        columns = []
        for b in range(C):
            low = r.kv[b, i, 0, pl.ds(tail, 16), :].astype(F32)
            flags = low[piece - tail : piece - tail + 1, :]
            flag = jnp.sum(jnp.where(row == lane, flags, 0.0), axis=1, keepdims=True)
            columns.append(jnp.where(lane1 == 0, (flag - 1.0) * BIG, 0.0).astype(BF))
        pick = lax.broadcasted_iota(jnp.int32, (16, 128), 1)
        pick = jnp.where(pick == 0, 1.0, 0.0).astype(BF)
        return dot_nt(pick, jnp.concatenate(columns, axis=0))[0:1, :]

    def attention(i):
        kv_far[i].wait_recv()
        kv_mate[i].wait_recv()
        k, v = all_keys(i)
        bias = key_bias(i)
        q = r.q[i].astype(F32)

        def head(h, total):
            mine = lane_head == h
            qh = jnp.where(mine, q, 0.0).astype(BF)
            scores = dot_nt(qh, k) * scale + bias
            top = jnp.max(scores, axis=-1, keepdims=True)
            e = jnp.exp(scores - top)
            w = (e * (1.0 / jnp.sum(e, axis=-1, keepdims=True))).astype(BF)
            r.wts[i, pl.ds(aligned(h * R, R), R), :] = w
            return jnp.where(mine, dot(w, v), total)

        total = lax.fori_loop(0, heads, head, jnp.zeros((R, W), F32))
        r.att[i] = total.astype(BF)

    H = 2
    halves = [pl.ds(j * (R // H), R // H) for j in range(H)]
    hop0, hop1, hop2 = {}, {}, {}

    def sum_plan(k, i):
        own = (r.own1, r.own2, r.own3, r.own4)[k - 1]
        tot = (r.tot1, r.tot2, r.tot3, r.tot4)[k - 1]
        in0 = (r.in01, r.in02, r.in03, r.in01)[k - 1]
        in1 = (r.in11, r.in12, r.in13, r.in11)[k - 1]
        for j, w in enumerate(halves):
            hop0[k, i, j] = net.remote(own.at[i, w], in0.at[i, w], (s, c, tmate))
            hop1[k, i, j] = net.remote(own.at[i, w], in1.at[i, w], (s, c, tpeer))
            hop2[k, i, j] = net.remote(tot.at[i, w], tot.at[i, w], (s, c, tmate))
        return own, tot, in0, in1

    sums = {(k, i): sum_plan(k, i) for k in range(1, 5) for i in range(I)}

    def add_rows(dst, a, b, i, j):
        def step(n, _):
            w = pl.ds(aligned(j * (R // H) + n * 16, 16), 16)
            dst[i, w, :] = (a[i, w, :].astype(F32) + b[i, w, :].astype(F32)).astype(BF)
            return 0

        lax.fori_loop(0, R // H // 16, step, 0)

    def sum_start(k, i):
        @pl.when(edge)
        def _():
            for j in range(H):
                hop0[k, i, j].start()

    def sum_mid(k, i):
        own, tot, in0, in1 = sums[k, i]

        @pl.when(inner)
        def _():
            for j in range(H):
                hop0[k, i, j].wait_recv()
                add_rows(own, own, in0, i, j)
                hop1[k, i, j].start()

    def sum_end(k, i):
        own, tot, in0, in1 = sums[k, i]

        @pl.when(inner)
        def _():
            for j in range(H):
                hop1[k, i, j].wait_recv()
                add_rows(tot, own, in1, i, j)
                hop2[k, i, j].start()

        @pl.when(edge)
        def _():
            for j in range(H):
                hop2[k, i, j].wait_recv()

    def attn_part(i):
        def tile(w):
            r.own1[i, :, w] = dot(r.att[i], r.wout[:, w]).astype(BF)

        tiles(D, tile)

    for i in range(I):
        kv_across[i].wait_recv()
        go(kv_far[i])
    weight_ready(OUT)
    for i in range(I):
        attention(i)
        attn_part(i)
        sum_start(1, i)
        if i:
            sum_mid(1, i - 1)
    sum_mid(1, I - 1)
    pass_on(UP)
    pass_on(DN)
    for i in range(I):
        loads["cot", i].wait()
        clear_tail(r.cot, i)

    def middle_of(i):
        def rows(w):
            x = r.tok[i, w, :].astype(F32) + r.tot1[i, w, :].astype(F32) + r.bout[...]
            r.middle[i, w, :] = x
            unit, _ = norm_stats(x)
            r.second[i, w, :] = (unit * r.g2[...] + r.b2[...]).astype(BF)

        blocks(rows)

    def feed_forward(i):
        def tile(w):
            u = dot(r.second[i], r.wup[:, w]) + r.bup[:, w]
            phi = 0.5 * (1.0 + lax.erf(u * 0.7071067811865476))
            r.activ[i, :, w] = (u * phi).astype(BF)
            slope = phi + u * jnp.exp(-0.5 * u * u) * 0.3989422804014327
            g = dot_nt(r.cot[i], r.wdn[w, :]) * slope
            r.actlow[i, :, w] = g.astype(BF)
            r.acc[6, :, w] += fold8(g)

        tiles(F, tile)

    def norm2_part(i):
        def tile(w):
            r.own3[i, :, w] = dot_nt(r.actlow[i], r.wup[w, :]).astype(BF)

        tiles(D, tile)

    def out_part(i):
        def tile(w):
            r.own2[i, :, w] = dot(r.activ[i], r.wdn[:, w]).astype(BF)

        tiles(D, tile)

    for i in range(I):
        sum_end(1, i)
        middle_of(i)
        if i == 0:
            weight_ready(UP)
            weight_ready(DN)
        feed_forward(i)
        norm2_part(i)
        sum_start(3, i)
        if i:
            sum_mid(3, i - 1)
    sum_mid(3, I - 1)
    for i in range(I):
        out_part(i)
        sum_start(2, i)

    grads = {
        QKV: (r.gqkv, r.r1qkv, r.r2qkv, r.r3qkv, r.fqkv),
        OUT: (r.gout, r.r1out, r.r2out, r.r3out, r.fout),
        UP: (r.gup, r.r1up, r.r2up, r.r3up, r.fup),
        DN: (r.gdn, r.r1dn, r.r2dn, r.r3dn, r.fdn),
    }

    def lanes_half(name):
        return name in (QKV, UP)

    def whole_half(name, ref, half):
        n = {QKV: W, UP: F, OUT: W, DN: F}[name] // 2
        w = pl.ds(aligned(half * n, n), n)
        if name == QKV:
            return ref.at[:, :, w]
        if name == UP:
            return ref.at[:, w]
        return ref.at[w, :]

    def shard_part(name, ref, shard):
        w = pl.ds(aligned(shard * part, part), part)
        if name == QKV:
            return ref.at[:, w, :]
        if name == UP:
            return ref.at[w, :]
        return ref.at[:, w]

    def add_into(dst, a, b):
        shape = dst.shape
        planes = shape[0] if len(shape) == 3 else 1
        n = shape[-2]
        for pln in range(planes):
            pick = (lambda ref: ref.at[pln]) if len(shape) == 3 else (lambda ref: ref)
            da, aa, bb = pick(dst), pick(a), pick(b)

            def step(k, _):
                w = pl.ds(aligned(k * RB, RB), RB)
                da[w, :] = (aa[w, :].astype(F32) + bb[w, :].astype(F32)).astype(BF)
                return 0

            lax.fori_loop(0, n // RB, step, 0)

    red = {}

    def reduce1(name):
        g, r1, r2, r3, f = grads[name]
        red[name, 1] = net.remote(whole_half(name, g, 1 - core), r1, on_mate)
        go(red[name, 1])

    def reduce2(name):
        g, r1, r2, r3, f = grads[name]
        red[name, 1].wait_recv()
        add_into(r1, whole_half(name, g, core), r1)
        for ds in range(1, S):
            to = lax.rem(s + ds, S)
            red[name, 2, ds] = net.remote(shard_part(name, r1, to), r2.at[ds], (to, c, t))
            go(red[name, 2, ds])

    def reduce3(name):
        g, r1, r2, r3, f = grads[name]
        for ds in range(1, S):
            red[name, 2, ds].wait_recv()
            first = shard_part(name, r1, s) if ds == 1 else r2.at[0]
            add_into(r2.at[0], first, r2.at[ds])
        red[name, 3] = net.remote(r2.at[0], r3, on_across)
        go(red[name, 3])

    def reduce4(name):
        g, r1, r2, r3, f = grads[name]
        red[name, 3].wait_recv()
        mine = whole_half(name, f, core)
        add_into(mine, r2.at[0], r3)
        red[name, 4] = net.remote(mine, mine, on_mate)
        go(red[name, 4])

    def flat(ref, w=None):
        v = ref[...] if w is None else ref[:, :, w]
        return v.reshape(I * R, v.shape[-1])

    def grad_down():
        def tile(w):
            r.gdn[w, :] = dot_tn(flat(r.activ, w), flat(r.cot)).astype(BF)

        tiles(F, tile)

    def grad_up():
        def tile(w):
            r.gup[w, :] = dot_tn(flat(r.second, w), flat(r.actlow)).astype(BF)

        tiles(D, tile)

    def grad_out():
        r.gout[...] = dot_tn(flat(r.att), flat(r.mlow)).astype(BF)

    def grad_qkv():
        def tile(w):
            x = flat(r.first, w)
            for n in range(3):
                r.gqkv[n, w, :] = dot_tn(x, flat(r.pg.at[n])).astype(BF)

        tiles(D, tile)

    grad_down()
    reduce1(DN)
    grad_up()
    reduce1(UP)
    reduce2(DN)
    reduce2(UP)

    def middle_back(i):
        def rows(w):
            unit, inv = norm_stats(r.middle[i, w, :])
            n2 = r.tot3[i, w, :].astype(F32)
            up = r.cot[i, w, :].astype(F32)
            g = up + norm_back(n2, unit, inv, r.g2[...])
            r.mgrad[i, w, :] = g
            r.mlow[i, w, :] = g.astype(BF)
            r.acc[1] += fold8(g)
            r.acc[4] += fold8(n2 * unit)
            r.acc[5] += fold8(n2)
            r.acc[7] += fold8(up)

        blocks(rows)

    def attention_back(i):
        k, v = all_keys(i)
        q = r.q[i].astype(F32)
        grad = dot_nt(r.mlow[i], r.wout[...])
        grad = grad.astype(BF).astype(F32)

        def head(h, total):
            mine = lane_head == h
            w = pl.ds(aligned(h * R, R), R)
            gh = jnp.where(mine, grad, 0.0).astype(BF)
            r.ost[w, :] = gh
            r.qst[w, :] = jnp.where(mine, q, 0.0).astype(BF)
            wg = dot_nt(gh, v)
            p = r.wts[i, w, :].astype(F32)
            pw = p * wg
            row_dot = jnp.sum(pw, axis=-1, keepdims=True)
            ds = ((pw - p * row_dot) * scale).astype(BF)
            r.dss[w, :] = ds
            return jnp.where(mine, dot(ds, k), total)

        dq = lax.fori_loop(0, heads, head, jnp.zeros((R, W), F32))
        r.acc[0, :, 0:W] += fold8(dq)
        r.pg[0, i] = dq.astype(BF)
        dk = dot_tn(r.dss[...], r.qst[...]).astype(BF)
        dv = dot_tn(r.wts[i], r.ost[...]).astype(BF)
        for b in range(C):
            r.dkv[b, i, 0] = dk[b * R : (b + 1) * R, :]
            r.dkv[b, i, 1] = dv[b * R : (b + 1) * R, :]

    back_mate, back_far, back_across = {}, {}, {}

    def key_send(i):
        back_far[i] = net.remote(r.dkv.at[far, i], r.rxa.at[1, i], on_mate)
        back_mate[i] = net.remote(r.dkv.at[mate, i], r.rxa.at[0, i], on_mate)
        go(back_far[i])
        go(back_mate[i])

    def key_mid(i):
        back_far[i].wait_recv()
        for n in range(2):
            both = r.dkv[across, i, n].astype(F32) + r.rxa[1, i, n].astype(F32)
            r.rxa[1, i, n] = both.astype(BF)
        back_across[i] = net.remote(r.rxa.at[1, i], r.rxb.at[i], on_across)
        go(back_across[i])

    def key_end(i):
        back_mate[i].wait_recv()
        back_across[i].wait_recv()
        for n in range(2):
            both = r.dkv[c, i, n].astype(F32) + r.rxa[0, i, n].astype(F32)
            both = both + r.rxb[i, n].astype(F32)
            r.pg[1 + n, i] = both.astype(BF)
            if n == 1:
                r.acc[0, :, W : 2 * W] += fold8(both)

    def norm1_part(i):
        def tile(w):
            total = dot_nt(r.pg[0, i], r.wqkv[0, w, :])
            total = total + dot_nt(r.pg[1, i], r.wqkv[1, w, :])
            total = total + dot_nt(r.pg[2, i], r.wqkv[2, w, :])
            r.own4[i, :, w] = total.astype(BF)

        tiles(D, tile)

    for i in range(I):
        sum_end(3, i)
        middle_back(i)
        attention_back(i)
        key_send(i)
        key_mid(i)
        sum_mid(2, i)
    for i in range(I):
        key_end(i)
        norm1_part(i)
        sum_start(4, i)
        if i:
            sum_mid(4, i - 1)
    sum_mid(4, I - 1)
    grad_out()
    reduce1(OUT)
    grad_qkv()
    reduce1(QKV)
    reduce3(DN)
    reduce3(UP)
    reduce2(OUT)
    reduce2(QKV)

    puts = []

    def out_rows(i):
        def rows(w):
            x = r.middle[i, w, :] + r.tot2[i, w, :].astype(F32) + r.bdn[...]
            r.middle[i, w, :] = x

        blocks(rows)
        put = net.local(r.middle.at[i, pl.ds(0, piece)], r.out_h.at[i])
        put.start()
        puts.append(put)

    def token_rows(i):
        def rows(w):
            unit, inv = norm_stats(r.tok[i, w, :].astype(F32))
            n1 = r.tot4[i, w, :].astype(F32)
            g = r.mgrad[i, w, :] + norm_back(n1, unit, inv, r.g1[...])
            r.mgrad[i, w, :] = g
            r.acc[2] += fold8(n1 * unit)
            r.acc[3] += fold8(n1)

        blocks(rows)
        put = net.local(r.mgrad.at[i, pl.ds(0, piece)], r.gtok_h.at[i])
        put.start()
        puts.append(put)

    for i in range(I):
        sum_end(2, i)
        out_rows(i)
    reduce4(DN)
    reduce4(UP)
    reduce3(OUT)
    reduce3(QKV)
    for i in range(I):
        sum_end(4, i)
        token_rows(i)

    for k in range(8):
        r.sm[k : k + 1, :] = jnp.sum(r.acc[k], axis=0, keepdims=True)
    slot = s * C + c
    r.smx[slot] = r.sm[...]
    small = []
    for ds in range(S):
        for dc in range(C):
            if ds or dc:
                to = (lax.rem(s + ds, S), lax.rem(c + dc, C), t)
                copy = net.remote(r.sm, r.smx.at[slot], to)
                go(copy)
                small.append(copy)
    reduce4(OUT)
    reduce4(QKV)
    for copy in small:
        copy.wait_recv()

    def add_slot(n, total):
        return total + r.smx[n]

    r.smo[...] = lax.fori_loop(1, S * C, add_slot, r.smx[0])
    for name in grads:
        red[name, 4].wait_recv()
    for put in puts:
        put.wait()
    for _, copy in sent:
        copy.wait_send()

    @pl.when(edge)
    def _():
        for copy in hop0.values():
            copy.wait_send()

    @pl.when(inner)
    def _():
        for copy in hop1.values():
            copy.wait_send()
        for copy in hop2.values():
            copy.wait_send()


def call_kernel(d, ins):
    scratch = scratch_of(d)
    I, D, W, F = d.images, d.width, d.local, d.hidden
    vmem = pl.BlockSpec(memory_space=pltpu.VMEM)
    hbm = pl.BlockSpec(memory_space=pl.ANY)
    arr = jax.ShapeDtypeStruct
    outs = dict(
        out_h=arr((I, d.piece, D), F32),
        gtok_h=arr((I, d.piece, D), F32),
        fqkv=arr((3, d.part, W), BF),
        fout=arr((W, d.part), BF),
        fup=arr((d.part, F), BF),
        fdn=arr((F, d.part), BF),
        smo=arr((8, D), F32),
    )
    names = (*ins, *outs, *scratch)
    return pl.pallas_call(
        functools.partial(body_kernel, d, names),
        out_shape=tuple(outs.values()),
        in_specs=[hbm] * 6 + [vmem] * 9,
        out_specs=(hbm, hbm, vmem, vmem, vmem, vmem, vmem),
        scratch_shapes=list(scratch.values()),
        compiler_params=pltpu.CompilerParams(
            collective_id=0, has_side_effects=True, vmem_limit_bytes=67043328
        ),
        name="encoder_layer",
    )(*ins.values())


def body(mesh, tokens, pad_mask, ln1_gain, ln1_shift, w_qkv, b_qv, w_out, b_out, ln2_gain, ln2_shift, w_up, b_up, w_down, b_down, cotangent):
    d = dims_of(mesh, tokens.shape, w_out.shape, w_up.shape)
    row = lambda v: v.reshape(1, -1)
    ins = dict(
        tok_h=tokens,
        cot_h=cotangent,
        wqkv_h=w_qkv,
        wout_h=w_out,
        wup_h=w_up,
        wdn_h=w_down,
        mask=pad_mask,
        g1=row(ln1_gain),
        b1=row(ln1_shift),
        bqv=b_qv,
        bout=row(b_out),
        g2=row(ln2_gain),
        b2=row(ln2_shift),
        bup=row(b_up),
        bdn=row(b_down),
    )
    out, gtok, fqkv, fout, fup, fdn, small = call_kernel(d, ins)
    W = d.local
    return (
        out,
        gtok,
        fqkv.astype(F32),
        small[0, : 2 * W].reshape(2, W),
        fout.astype(F32),
        small[1],
        small[2],
        small[3],
        small[4],
        small[5],
        fup.astype(F32),
        small[6, : d.hidden],
        fdn.astype(F32),
        small[7],
    )


def solution(mesh):
    return jax.shard_map(
        functools.partial(body, mesh),
        mesh=mesh,
        in_specs=(
            P("shard", "ctx", None),
            P("shard", "ctx"),
            P(),
            P(),
            P(None, "shard", "tp"),
            P(None, "tp"),
            P("tp", "shard"),
            P(),
            P(),
            P(),
            P("shard", "tp"),
            P("tp"),
            P("tp", "shard"),
            P(),
            P("shard", "ctx", None),
        ),
        out_specs=(
            P("shard", "ctx", None),
            P("shard", "ctx", None),
            P(None, "shard", "tp"),
            P(None, "tp"),
            P("tp", "shard"),
            P(),
            P(),
            P(),
            P(),
            P(),
            P("shard", "tp"),
            P("tp"),
            P("tp", "shard"),
            P(),
        ),
        check_vma=False,
    )
```

time: 628 us -> 233 us (0.37)
  waiting for transfers between devices: 430 us -> 0 us
  Pallas kernels: 0 us -> 219 us
  blocking collectives: 66.3 us -> 0 us
  matrix products: 54.6 us -> 0 us
  other arithmetic: 32.1 us -> 6.53 us
  local copies, waits for them, and re-layouts: 27.5 us -> 6.57 us
  between operations: 15.3 us -> 0.68 us
    pallas_call x0 -> x1, Pallas kernels: none -> 219 us  [call_kernel(): pl.pallas_call(functools.partial(body_kernel, d, names), out_shape=tuple(...]
    psum x4 -> x0, waiting for transfers between devices: 215 us -> none  [the longest x1 80.3 us: body(): lax.psum(mlp_part.astype(jnp.bfloat16), 'tp').astype(jnp.float32)]
    reduce_scatter x4 -> x0, waiting for transfers between devices: 105 us -> none  [the longest x1 34.8 us: body(): lax.psum_scatter(summed[3].astype(jnp.bfloat16), 'shard', scatter_dimensi...]
    all_gather x3 -> x0, waiting for transfers between devices: 67.8 us -> none  [the longest x1 30.7 us: body(): lax.all_gather(w_up, 'shard', axis=0, tiled=True)]
    dot_general x18 -> x0, matrix products: 54.6 us -> none  [the longest x1 7.82 us: body(): jnp.dot(second_low, up_full, preferred_element_type=jnp.float32) + b_up]
    all_gather x4 -> x0, blocking collectives: 42.1 us -> none  [the longest x1 14.5 us: body(): lax.all_gather(w_out, 'shard', axis=1, tiled=True)]
    unnamed x13 -> x0, waiting for transfers between devices: 41.7 us -> none
    psum x1 -> x0, blocking collectives: 24.2 us -> none  [body(): lax.psum((jnp.stack([jnp.sum(query_grad, axis=0), jnp.sum(value_grad, axi...]
  transfers between devices with their start and end apart: 12 -> 0, of which waited for: 12 -> 0; matrix products, arithmetic and copies ran while one was open for 8% -> 0% of each run, Pallas kernels for 0% -> 0%
where the time goes in v1:
time: 233 us
  Pallas kernels  219 us (94%)
  local copies, waits for them, and re-layouts  6.57 us (3%)
  other arithmetic  6.53 us (3%)
    pallas_call x1, Pallas kernels, call_kernel(): pl.pallas_call(functools.partial(body_kernel, d, names), out_shape=tuple(...  219 us

profile of v1, /device:TPU:0, one launch (start us, length us, event | category | flops | bytes accessed | tf_op | source)
XLA Modules:
  0.0 233.0 jit_solution(17108966371813928009)
XLA Ops:
  0.7 219.2 %encoder_layer.1 = (f32[3,152,1024]{2,1,0:T(8,128)}, f32[3,152,1024]{2,1,0:T(8,128)}, bf16[3,512,256]{2,1,0:T(8,128)(2,1)}, bf16[256,512]{1,0:T(8,128)(2,1)}, bf...) custom-call(bf16[3,152,1024]{2,1,0:T(8,128)(2,1)} %refs_0_.1, ...), custom_call_target="tpu_custom_call" | custom-call | tf_op jit(solution)/shard_map/encoder_layer/pallas_call | solution.py:806
  219.9 0.0 copy-start.2
  219.9 1.8 fusion
  221.7 0.7 slice_reduce_fusion
  222.4 0.6 reshape_squeeze.3
  223.0 2.8 %convert_element_type.14 = f32[512,1024]{1,0:T(8,128)} convert(bf16[512,1024]{1,0:T(8,128)(2,1)} %get-tuple-element.26) | non-fusion elementwise | flops 524288 | bytes 3145728 | tf_op jit(solution)/shard_map/convert_element_type | solution.py:852
  225.8 0.0 copy-start.3
  225.8 0.0 copy-done.2
  225.8 1.6 convert_element_type.15
  227.4 0.0 copy-start.4
  227.4 0.0 copy-start.1
  227.4 0.0 copy-done.3
  227.4 1.3 convert_element_type.12
  228.7 0.0 copy-done.4
  228.7 0.9 convert_element_type.13
  229.5 0.0 copy-done.1
  229.6 0.0 copy-start
  229.6 1.2 copy.31
  230.8 0.9 copy-done
  231.8 1.2 copy.32
Async XLA Ops:
  219.9 5.9 %copy-start.2 = (bf16[1024,512]{1,0:T(8,128)(2,1)S(1)}, bf16[1024,512]{1,0:T(8,128)(2,1)}, u32[]{:S(2)}) copy-start(bf16[1024,512]{1,0:T(8,128)(2,1)} %get-tuple-element.27) | copy-start | bytes 3145732
  225.8 1.6 copy-start.3
  227.4 1.3 copy-start.4
  227.4 2.2 copy-start.1
  229.6 2.2 copy-start

commit v2 on v1

--- a/solution.py
+++ b/solution.py
@@ -17,6 +17,38 @@
 TILE = 256
 
 
+KV, Q, OUT, UP, DN = range(5)
+Q0, K0, V0, OUT0, UP0, UP1, DN0, DN1 = range(8)
+PIECES = (DN0, DN1, UP0, UP1, OUT0, Q0, K0, V0)
+(
+    LN, FW, KVP, QP, KF, AT, P1, SS, SJ, SM, SE, MO, FF, P3, P2, MB, AB, KM, KE, P4, OR, TR,
+    GD, GU, GO, GQ, R2, R3, R4, SMA, SMB, FIN,
+) = range(32)
+CUTS = ((0, 80), (80, 72))
+ORDER = (
+    (LN, 2), (LN, 0), (LN, 1), (FW, KV), (KVP, 0), (FW, Q), (QP, 1), (QP, 2), (KVP, 1), (KVP, 2),
+    (KF, 0), (QP, 0), (FW, OUT), (AT, 0), (P1, 0), (SS, 1, 0), (KF, 1), (AT, 1), (KF, 2), (P1, 1),
+    (SM, 1, 0, 0), (SS, 1, 1), (AT, 2), (SM, 1, 0, 1), (SE, 1, 0, 0), (SM, 1, 1, 0), (FW, UP),
+    (SE, 1, 0, 1), (P1, 2), (SM, 1, 1, 1), (SS, 1, 2), (FW, DN), (MO, 0), (SE, 1, 1, 0),
+    (SM, 1, 2, 0), (FF, 0), (P3, 0), (SE, 1, 1, 1), (SM, 1, 2, 1), (SS, 3, 0), (MO, 1), (FF, 1),
+    (SE, 1, 2, 0), (P3, 1), (SS, 3, 1), (P2, 0), (SE, 1, 2, 1), (MO, 2), (SM, 3, 0, 0), (FF, 2),
+    (P3, 2), (SM, 3, 0, 1), (SS, 3, 2), (GD,), (SJ, 2, 0, 1), (SE, 3, 0, 0), (P2, 1), (SM, 3, 1, 0),
+    (SJ, 2, 1, 0), (GU,), (SE, 3, 0, 1), (SM, 3, 1, 1), (R2, DN0), (P2, 2), (MB, 0), (SE, 3, 1, 0),
+    (SM, 3, 2, 0), (AB, 0), (SM, 3, 2, 1), (SE, 3, 1, 1), (SJ, 2, 2, 1), (KM, 0), (R3, DN0),
+    (R2, DN1), (SJ, 2, 1, 1), (MB, 1), (SJ, 2, 0, 0), (SM, 2, 0, 1), (SE, 3, 2, 0), (AB, 1),
+    (SE, 3, 2, 1), (R2, UP1), (SM, 2, 1, 0), (KE, 0), (R2, UP0), (P4, 0), (KM, 1), (SE, 2, 0, 1),
+    (SM, 2, 2, 1), (MB, 2), (SS, 4, 0), (R3, DN1), (SM, 2, 1, 1), (SE, 2, 1, 0), (AB, 2),
+    (SE, 2, 2, 1), (SM, 2, 0, 0), (KE, 1), (P4, 1), (SS, 4, 1), (KM, 2), (GO,), (SM, 4, 0, 0),
+    (SE, 2, 1, 1), (GQ, 0), (R3, UP0), (OR, 1), (R4, DN1), (R2, Q0), (SM, 4, 0, 1), (R3, UP1),
+    (SE, 2, 0, 0), (KE, 2), (P4, 2), (SM, 4, 1, 0), (SS, 4, 2), (GQ, 2), (SE, 4, 0, 0), (OR, 0),
+    (R2, OUT0), (GQ, 1), (SJ, 2, 2, 0), (R3, Q0), (SE, 4, 0, 1), (R2, K0), (SM, 4, 1, 1), (R4, UP0),
+    (TR, 0), (SE, 4, 1, 0), (R2, V0), (SM, 4, 2, 0), (SE, 4, 1, 1), (R3, K0), (SM, 4, 2, 1),
+    (R4, Q0), (SMA,), (TR, 1), (R3, OUT0), (SE, 4, 2, 0), (R3, V0), (R4, DN0), (SM, 2, 2, 0),
+    (SE, 4, 2, 1), (SE, 2, 2, 0), (R4, UP1), (R4, OUT0), (TR, 2), (SMB,), (R4, K0), (R4, V0),
+    (OR, 2), (FIN,),
+)
+
+
 def dot(a, b):
     return lax.dot_general(a, b, (((1,), (0,)), ((), ())), preferred_element_type=F32)
 
@@ -48,6 +80,10 @@
 
 def aligned(i, m):
     return pl.multiple_of(i, m)
+
+
+def span(i, n):
+    return pl.ds(aligned(i * n, n), n)
 
 
 class Dims:
@@ -65,10 +101,8 @@
     d.hidden = w_up[1]
     d.heads = d.local // HD
     d.keys = d.C * d.rows
+    assert d.rows > d.piece
     return d
-
-
-KV, Q, OUT, UP, DN, QKV = range(6)
 
 
 def scratch_of(d):
@@ -108,18 +142,33 @@
         gout=bf(W, D),
         gup=bf(D, F),
         gdn=bf(F, D),
-        r1qkv=bf(3, D, W // 2),
-        r1out=bf(W // 2, D),
-        r1up=bf(D, F // 2),
-        r1dn=bf(F // 2, D),
-        r2qkv=bf(S, 3, D // S, W // 2),
-        r2out=bf(S, W // 2, D // S),
-        r2up=bf(S, D // S, F // 2),
-        r2dn=bf(S, F // 2, D // S),
-        r3qkv=bf(3, D // S, W // 2),
-        r3out=bf(W // 2, D // S),
-        r3up=bf(D // S, F // 2),
-        r3dn=bf(F // 2, D // S),
+        r1q=bf(3, D, W // 2),
+        r1o=bf(W // 2, D),
+        r1u=bf(2, D, F // 4),
+        r1d=bf(2, F // 4, D),
+        r2q=bf(3, S, D // S, W // 2),
+        r2o=bf(S, W // 2, D // S),
+        r2u=bf(2, S, D // S, F // 4),
+        r2d=bf(2, S, F // 4, D // S),
+        r3q=bf(3, D // S, W // 2),
+        r3o=bf(W // 2, D // S),
+        r3u=bf(2, D // S, F // 4),
+        r3d=bf(2, F // 4, D // S),
+        fqkv=bf(3, D // S, W),
+        fout=bf(W, D // S),
+        fup=bf(D // S, F),
+        fdn=bf(F, D // S),
+        mask=pltpu.VMEM((I, d.piece), jnp.int32),
+        g1=f32(1, D),
+        b1=f32(1, D),
+        bqv=f32(2, W),
+        bout=f32(1, D),
+        g2=f32(1, D),
+        b2=f32(1, D),
+        bup=f32(1, F),
+        bdn=f32(1, D),
+        smt=f32(8, D // 4),
+        smtx=f32(S * C, 8, D // 4),
     )
     full = lambda: bf(I, R, D)
     scratch.update(own1=full(), own2=full(), own3=full(), own4=full())
@@ -132,7 +181,7 @@
     return scratch
 
 
-MAX_COPIES = 200
+MAX_COPIES = 320
 
 
 class Net:
@@ -179,31 +228,58 @@
         copy.start()
         sent.append((None, copy))
 
+    tail = piece // 16 * 16
+    for ref in (r.tot1, r.tot2, r.tot3, r.tot4, r.in01, r.in02, r.in03, r.in11, r.in12, r.in13):
+        for i in range(I):
+            ref[i, tail:R, :] = jnp.zeros((R - tail, D), BF)
+    for i in range(I):
+        for n in range(2):
+            r.rxb[i, n, tail:R, :] = jnp.zeros((R - tail, W), BF)
+            for b in range(2):
+                r.rxa[b, i, n, tail:R, :] = jnp.zeros((R - tail, W), BF)
+
+    barrier = pltpu.get_barrier_semaphore()
+    pl.semaphore_signal(barrier, inc=1, device_id=(s, c, tmate), device_id_type=MESH)
+    for ds in range(S):
+        for dc in range(C):
+            if ds or dc:
+                where = (lax.rem(s + ds, S), lax.rem(c + dc, C), t)
+                pl.semaphore_signal(barrier, inc=1, device_id=where, device_id_type=MESH)
+
+    @pl.when(inner)
+    def _():
+        pl.semaphore_signal(barrier, inc=1, device_id=(s, c, tpeer), device_id_type=MESH)
+
     loads = {}
     for i in range(I):
-        loads["tok", i] = net.local(r.tok_h.at[i], r.tok.at[i, pl.ds(0, piece)])
-    rows_s = pl.ds(aligned(s * part, part), part)
+        loads[LN, i] = net.local(r.tok_h.at[i], r.tok.at[i, pl.ds(0, piece)])
+    vectors = [
+        net.local(a, b)
+        for a, b in (
+            (r.mask_h, r.mask),
+            (r.g1_h, r.g1),
+            (r.b1_h, r.b1),
+            (r.bqv_h, r.bqv),
+            (r.bout_h, r.bout),
+            (r.g2_h, r.g2),
+            (r.b2_h, r.b2),
+            (r.bup_h, r.bup),
+            (r.bdn_h, r.bdn),
+        )
+    ]
+    rows_s = span(s, part)
     loads[KV] = net.local(r.wqkv_h.at[pl.ds(1, 2)], r.wqkv.at[pl.ds(1, 2), rows_s])
     loads[Q] = net.local(r.wqkv_h.at[pl.ds(0, 1)], r.wqkv.at[pl.ds(0, 1), rows_s])
     loads[OUT] = net.local(r.wout_h, r.wout.at[:, rows_s])
     loads[UP] = net.local(r.wup_h, r.wup.at[rows_s])
     loads[DN] = net.local(r.wdn_h, r.wdn.at[:, rows_s])
     for i in range(I):
-        loads["cot", i] = net.local(r.cot_h.at[i], r.cot.at[i, pl.ds(0, piece)])
-    for copy in loads.values():
+        loads[FF, i] = net.local(r.cot_h.at[i], r.cot.at[i, pl.ds(0, piece)])
+    for copy in (*loads.values(), *vectors):
         copy.start()
-
-    barrier = pltpu.get_barrier_semaphore()
-    for ds in range(S):
-        for dc in range(C):
-            if ds or dc:
-                where = (lax.rem(s + ds, S), lax.rem(c + dc, C), t)
-                pl.semaphore_signal(barrier, inc=1, device_id=where, device_id_type=MESH)
-    pl.semaphore_signal(barrier, inc=1, device_id=(s, c, tmate), device_id_type=MESH)
 
     @pl.when(inner)
     def _():
-        pl.semaphore_signal(barrier, inc=1, device_id=(s, c, tpeer), device_id_type=MESH)
         pl.semaphore_wait(barrier, S * C + 1)
 
     @pl.when(edge)
@@ -256,12 +332,15 @@
             gather[name, ds].wait_recv()
             go(spread[name, ds])
 
+    arrived = set()
+
     def weight_ready(name):
+        if name in arrived:
+            return
+        arrived.add(name)
         loads[name].wait()
         for ds in range(1, S):
             spread[name, ds].wait_recv()
-
-    tail = piece // 16 * 16
 
     def clear_tail(ref, i):
         if tail < R:
@@ -270,11 +349,13 @@
             ref[i, pl.ds(tail, R - tail), :] = jnp.where(row < piece - tail, old, 0.0).astype(BF)
 
     def blocks(fn):
+        n = R // 2
+
         def step(b, _):
-            fn(pl.ds(aligned(b * RB, RB), RB))
+            fn(span(b, n))
             return 0
 
-        lax.fori_loop(0, R // RB, step, 0)
+        lax.fori_loop(0, 2, step, 0)
 
     def tiles(n, fn):
         def step(b, _):
@@ -286,10 +367,12 @@
     r.acc[...] = jnp.zeros_like(r.acc)
     r.sm[...] = jnp.zeros_like(r.sm)
     r.maskw[...] = jnp.zeros_like(r.maskw)
+    for copy in vectors:
+        copy.wait()
     r.maskw[0:I, 0:piece] = (r.mask[...] > 0).astype(F32)
 
     def first_norm(i):
-        loads["tok", i].wait()
+        loads[LN, i].wait()
         clear_tail(r.tok, i)
 
         def rows(w):
@@ -298,15 +381,11 @@
 
         blocks(rows)
 
-    for i in range(I):
-        first_norm(i)
-    pass_on(KV)
-    weight_ready(KV)
-
     kv_mate, kv_across, kv_far = {}, {}, {}
     row_w = lax.broadcasted_iota(jnp.int32, (R, W), 0)
 
     def keys_values(i):
+        weight_ready(KV)
         x = r.first[i]
         key = dot(x, r.wqkv[1])
         flags = jnp.broadcast_to(r.maskw[i : i + 1, :], (R, W))
@@ -320,13 +399,13 @@
         go(kv_across[i])
         go(kv_mate[i])
 
-    for i in range(I):
-        keys_values(i)
-    pass_on(Q)
-    weight_ready(Q)
-    for i in range(I):
+    def queries(i):
+        weight_ready(Q)
         r.q[i] = (dot(r.first[i], r.wqkv[0]) + r.bqv[0:1, :]).astype(BF)
-    pass_on(OUT)
+
+    def key_forward(i):
+        kv_across[i].wait_recv()
+        go(kv_far[i])
 
     lane_head = lax.broadcasted_iota(jnp.int32, (R, W), 1) // HD
     scale = 1.0 / math.sqrt(HD)
@@ -370,8 +449,6 @@
         total = lax.fori_loop(0, heads, head, jnp.zeros((R, W), F32))
         r.att[i] = total.astype(BF)
 
-    H = 2
-    halves = [pl.ds(j * (R // H), R // H) for j in range(H)]
     hop0, hop1, hop2 = {}, {}, {}
 
     def sum_plan(k, i):
@@ -379,7 +456,8 @@
         tot = (r.tot1, r.tot2, r.tot3, r.tot4)[k - 1]
         in0 = (r.in01, r.in02, r.in03, r.in01)[k - 1]
         in1 = (r.in11, r.in12, r.in13, r.in11)[k - 1]
-        for j, w in enumerate(halves):
+        for j, (first, n) in enumerate(CUTS):
+            w = pl.ds(first, n)
             hop0[k, i, j] = net.remote(own.at[i, w], in0.at[i, w], (s, c, tmate))
             hop1[k, i, j] = net.remote(own.at[i, w], in1.at[i, w], (s, c, tpeer))
             hop2[k, i, j] = net.remote(tot.at[i, w], tot.at[i, w], (s, c, tmate))
@@ -388,68 +466,61 @@
     sums = {(k, i): sum_plan(k, i) for k in range(1, 5) for i in range(I)}
 
     def add_rows(dst, a, b, i, j):
-        def step(n, _):
-            w = pl.ds(aligned(j * (R // H) + n * 16, 16), 16)
+        first, n = CUTS[j]
+
+        def step(m, _):
+            w = pl.ds(aligned(first + m * 16, 16), 16)
             dst[i, w, :] = (a[i, w, :].astype(F32) + b[i, w, :].astype(F32)).astype(BF)
             return 0
 
-        lax.fori_loop(0, R // H // 16, step, 0)
+        lax.fori_loop(0, -(-n // 16), step, 0)
+
+    def sum_block(k, i, j):
+        @pl.when(edge)
+        def _():
+            hop0[k, i, j].start()
 
     def sum_start(k, i):
         @pl.when(edge)
         def _():
-            for j in range(H):
+            for j in range(len(CUTS)):
                 hop0[k, i, j].start()
 
-    def sum_mid(k, i):
+    def sum_mid(k, i, j):
         own, tot, in0, in1 = sums[k, i]
 
         @pl.when(inner)
         def _():
-            for j in range(H):
-                hop0[k, i, j].wait_recv()
-                add_rows(own, own, in0, i, j)
-                hop1[k, i, j].start()
-
-    def sum_end(k, i):
+            hop0[k, i, j].wait_recv()
+            add_rows(own, own, in0, i, j)
+            hop1[k, i, j].start()
+
+    def sum_end(k, i, j):
         own, tot, in0, in1 = sums[k, i]
 
         @pl.when(inner)
         def _():
-            for j in range(H):
-                hop1[k, i, j].wait_recv()
-                add_rows(tot, own, in1, i, j)
-                hop2[k, i, j].start()
-
+            hop1[k, i, j].wait_recv()
+            add_rows(tot, own, in1, i, j)
+            hop2[k, i, j].start()
+
+    def sum_got(k, i):
         @pl.when(edge)
         def _():
-            for j in range(H):
+            for j in range(len(CUTS)):
                 hop2[k, i, j].wait_recv()
 
     def attn_part(i):
+        weight_ready(OUT)
+
         def tile(w):
             r.own1[i, :, w] = dot(r.att[i], r.wout[:, w]).astype(BF)
 
         tiles(D, tile)
 
-    for i in range(I):
-        kv_across[i].wait_recv()
-        go(kv_far[i])
-    weight_ready(OUT)
-    for i in range(I):
-        attention(i)
-        attn_part(i)
-        sum_start(1, i)
-        if i:
-            sum_mid(1, i - 1)
-    sum_mid(1, I - 1)
-    pass_on(UP)
-    pass_on(DN)
-    for i in range(I):
-        loads["cot", i].wait()
-        clear_tail(r.cot, i)
-
     def middle_of(i):
+        sum_got(1, i)
+
         def rows(w):
             x = r.tok[i, w, :].astype(F32) + r.tot1[i, w, :].astype(F32) + r.bout[...]
             r.middle[i, w, :] = x
@@ -459,6 +530,11 @@
         blocks(rows)
 
     def feed_forward(i):
+        weight_ready(UP)
+        weight_ready(DN)
+        loads[FF, i].wait()
+        clear_tail(r.cot, i)
+
         def tile(w):
             u = dot(r.second[i], r.wup[:, w]) + r.bup[:, w]
             phi = 0.5 * (1.0 + lax.erf(u * 0.7071067811865476))
@@ -482,96 +558,78 @@
 
         tiles(D, tile)
 
-    for i in range(I):
-        sum_end(1, i)
-        middle_of(i)
-        if i == 0:
-            weight_ready(UP)
-            weight_ready(DN)
-        feed_forward(i)
-        norm2_part(i)
-        sum_start(3, i)
-        if i:
-            sum_mid(3, i - 1)
-    sum_mid(3, I - 1)
-    for i in range(I):
-        out_part(i)
-        sum_start(2, i)
-
-    grads = {
-        QKV: (r.gqkv, r.r1qkv, r.r2qkv, r.r3qkv, r.fqkv),
-        OUT: (r.gout, r.r1out, r.r2out, r.r3out, r.fout),
-        UP: (r.gup, r.r1up, r.r2up, r.r3up, r.fup),
-        DN: (r.gdn, r.r1dn, r.r2dn, r.r3dn, r.fdn),
-    }
-
-    def lanes_half(name):
-        return name in (QKV, UP)
-
-    def whole_half(name, ref, half):
-        n = {QKV: W, UP: F, OUT: W, DN: F}[name] // 2
-        w = pl.ds(aligned(half * n, n), n)
-        if name == QKV:
-            return ref.at[:, :, w]
-        if name == UP:
-            return ref.at[:, w]
-        return ref.at[w, :]
-
-    def shard_part(name, ref, shard):
-        w = pl.ds(aligned(shard * part, part), part)
-        if name == QKV:
-            return ref.at[:, w, :]
-        if name == UP:
-            return ref.at[w, :]
-        return ref.at[:, w]
+    tall = (Q0, K0, V0, UP0, UP1)
+
+    def half_view(piece_id, half, planes, wo, up, dn):
+        if piece_id in (Q0, K0, V0):
+            return planes.at[piece_id, :, span(half, W // 2)]
+        if piece_id == OUT0:
+            return wo.at[span(half, W // 2), :]
+        n = F // 4
+        if piece_id in (UP0, UP1):
+            return up.at[:, pl.ds(aligned(half * 2 * n + (piece_id - UP0) * n, n), n)]
+        return dn.at[pl.ds(aligned(half * 2 * n + (piece_id - DN0) * n, n), n), :]
+
+    def grad_half(p, half):
+        return half_view(p, half, r.gqkv, r.gout, r.gup, r.gdn)
+
+    def final_half(p, half):
+        return half_view(p, half, r.fqkv, r.fout, r.fup, r.fdn)
+
+    def slot_of(p, q, o, u, d_):
+        if p in (Q0, K0, V0):
+            return q.at[p]
+        if p == OUT0:
+            return o
+        return u.at[p - UP0] if p in (UP0, UP1) else d_.at[p - DN0]
+
+    def shard_part(p, ref, shard):
+        w = span(shard, part)
+        return ref.at[w, :] if p in tall else ref.at[:, w]
 
     def add_into(dst, a, b):
-        shape = dst.shape
-        planes = shape[0] if len(shape) == 3 else 1
-        n = shape[-2]
-        for pln in range(planes):
-            pick = (lambda ref: ref.at[pln]) if len(shape) == 3 else (lambda ref: ref)
-            da, aa, bb = pick(dst), pick(a), pick(b)
-
-            def step(k, _):
-                w = pl.ds(aligned(k * RB, RB), RB)
-                da[w, :] = (aa[w, :].astype(F32) + bb[w, :].astype(F32)).astype(BF)
-                return 0
-
-            lax.fori_loop(0, n // RB, step, 0)
+        def step(k, _):
+            w = span(k, RB)
+            dst[w, :] = (a[w, :].astype(F32) + b[w, :].astype(F32)).astype(BF)
+            return 0
+
+        lax.fori_loop(0, dst.shape[0] // RB, step, 0)
 
     red = {}
 
-    def reduce1(name):
-        g, r1, r2, r3, f = grads[name]
-        red[name, 1] = net.remote(whole_half(name, g, 1 - core), r1, on_mate)
-        go(red[name, 1])
-
-    def reduce2(name):
-        g, r1, r2, r3, f = grads[name]
-        red[name, 1].wait_recv()
-        add_into(r1, whole_half(name, g, core), r1)
+    def reduce1(p):
+        red[p, 1] = net.remote(
+            grad_half(p, 1 - core), slot_of(p, r.r1q, r.r1o, r.r1u, r.r1d), on_mate
+        )
+        go(red[p, 1])
+
+    def reduce2(p):
+        r1, r2 = slot_of(p, r.r1q, r.r1o, r.r1u, r.r1d), slot_of(p, r.r2q, r.r2o, r.r2u, r.r2d)
+        red[p, 1].wait_recv()
+        add_into(r1, grad_half(p, core), r1)
         for ds in range(1, S):
             to = lax.rem(s + ds, S)
-            red[name, 2, ds] = net.remote(shard_part(name, r1, to), r2.at[ds], (to, c, t))
-            go(red[name, 2, ds])
-
-    def reduce3(name):
-        g, r1, r2, r3, f = grads[name]
+            red[p, 2, ds] = net.remote(shard_part(p, r1, to), r2.at[ds], (to, c, t))
+            go(red[p, 2, ds])
+
+    def reduce3(p):
+        r1, r2 = slot_of(p, r.r1q, r.r1o, r.r1u, r.r1d), slot_of(p, r.r2q, r.r2o, r.r2u, r.r2d)
         for ds in range(1, S):
-            red[name, 2, ds].wait_recv()
-            first = shard_part(name, r1, s) if ds == 1 else r2.at[0]
-            add_into(r2.at[0], first, r2.at[ds])
-        red[name, 3] = net.remote(r2.at[0], r3, on_across)
-        go(red[name, 3])
-
-    def reduce4(name):
-        g, r1, r2, r3, f = grads[name]
-        red[name, 3].wait_recv()
-        mine = whole_half(name, f, core)
-        add_into(mine, r2.at[0], r3)
-        red[name, 4] = net.remote(mine, mine, on_mate)
-        go(red[name, 4])
+            red[p, 2, ds].wait_recv()
+            mine = shard_part(p, r1, s) if ds == 1 else r2.at[0]
+            add_into(r2.at[0], mine, r2.at[ds])
+        red[p, 3] = net.remote(
+            r2.at[0], slot_of(p, r.r3q, r.r3o, r.r3u, r.r3d), on_across
+        )
+        go(red[p, 3])
+
+    def reduce4(p):
+        r2 = slot_of(p, r.r2q, r.r2o, r.r2u, r.r2d)
+        red[p, 3].wait_recv()
+        mine = final_half(p, core)
+        add_into(mine, r2.at[0], slot_of(p, r.r3q, r.r3o, r.r3u, r.r3d))
+        red[p, 4] = net.remote(mine, mine, on_mate)
+        go(red[p, 4])
 
     def flat(ref, w=None):
         v = ref[...] if w is None else ref[:, :, w]
@@ -582,32 +640,31 @@
             r.gdn[w, :] = dot_tn(flat(r.activ, w), flat(r.cot)).astype(BF)
 
         tiles(F, tile)
+        reduce1(DN0)
+        reduce1(DN1)
 
     def grad_up():
         def tile(w):
             r.gup[w, :] = dot_tn(flat(r.second, w), flat(r.actlow)).astype(BF)
 
         tiles(D, tile)
+        reduce1(UP0)
+        reduce1(UP1)
 
     def grad_out():
         r.gout[...] = dot_tn(flat(r.att), flat(r.mlow)).astype(BF)
-
-    def grad_qkv():
+        reduce1(OUT0)
+
+    def grad_proj(n):
         def tile(w):
-            x = flat(r.first, w)
-            for n in range(3):
-                r.gqkv[n, w, :] = dot_tn(x, flat(r.pg.at[n])).astype(BF)
+            r.gqkv[n, w, :] = dot_tn(flat(r.first, w), flat(r.pg.at[n])).astype(BF)
 
         tiles(D, tile)
-
-    grad_down()
-    reduce1(DN)
-    grad_up()
-    reduce1(UP)
-    reduce2(DN)
-    reduce2(UP)
+        reduce1(Q0 + n)
 
     def middle_back(i):
+        sum_got(3, i)
+
         def rows(w):
             unit, inv = norm_stats(r.middle[i, w, :])
             n2 = r.tot3[i, w, :].astype(F32)
@@ -650,12 +707,14 @@
         for b in range(C):
             r.dkv[b, i, 0] = dk[b * R : (b + 1) * R, :]
             r.dkv[b, i, 1] = dv[b * R : (b + 1) * R, :]
+        key_send(i)
 
     back_mate, back_far, back_across = {}, {}, {}
+    real = pl.ds(0, piece)
 
     def key_send(i):
-        back_far[i] = net.remote(r.dkv.at[far, i], r.rxa.at[1, i], on_mate)
-        back_mate[i] = net.remote(r.dkv.at[mate, i], r.rxa.at[0, i], on_mate)
+        back_far[i] = net.remote(r.dkv.at[far, i, :, real], r.rxa.at[1, i, :, real], on_mate)
+        back_mate[i] = net.remote(r.dkv.at[mate, i, :, real], r.rxa.at[0, i, :, real], on_mate)
         go(back_far[i])
         go(back_mate[i])
 
@@ -664,7 +723,7 @@
         for n in range(2):
             both = r.dkv[across, i, n].astype(F32) + r.rxa[1, i, n].astype(F32)
             r.rxa[1, i, n] = both.astype(BF)
-        back_across[i] = net.remote(r.rxa.at[1, i], r.rxb.at[i], on_across)
+        back_across[i] = net.remote(r.rxa.at[1, i, :, real], r.rxb.at[i, :, real], on_across)
         go(back_across[i])
 
     def key_end(i):
@@ -686,32 +745,11 @@
 
         tiles(D, tile)
 
-    for i in range(I):
-        sum_end(3, i)
-        middle_back(i)
-        attention_back(i)
-        key_send(i)
-        key_mid(i)
-        sum_mid(2, i)
-    for i in range(I):
-        key_end(i)
-        norm1_part(i)
-        sum_start(4, i)
-        if i:
-            sum_mid(4, i - 1)
-    sum_mid(4, I - 1)
-    grad_out()
-    reduce1(OUT)
-    grad_qkv()
-    reduce1(QKV)
-    reduce3(DN)
-    reduce3(UP)
-    reduce2(OUT)
-    reduce2(QKV)
-
     puts = []
 
     def out_rows(i):
+        sum_got(2, i)
+
         def rows(w):
             x = r.middle[i, w, :] + r.tot2[i, w, :].astype(F32) + r.bdn[...]
             r.middle[i, w, :] = x
@@ -722,6 +760,8 @@
         puts.append(put)
 
     def token_rows(i):
+        sum_got(4, i)
+
         def rows(w):
             unit, inv = norm_stats(r.tok[i, w, :].astype(F32))
             n1 = r.tot4[i, w, :].astype(F32)
@@ -735,56 +775,149 @@
         put.start()
         puts.append(put)
 
-    for i in range(I):
-        sum_end(2, i)
-        out_rows(i)
-    reduce4(DN)
-    reduce4(UP)
-    reduce3(OUT)
-    reduce3(QKV)
-    for i in range(I):
-        sum_end(4, i)
-        token_rows(i)
-
-    for k in range(8):
-        r.sm[k : k + 1, :] = jnp.sum(r.acc[k], axis=0, keepdims=True)
     slot = s * C + c
-    r.smx[slot] = r.sm[...]
     small = []
-    for ds in range(S):
-        for dc in range(C):
-            if ds or dc:
-                to = (lax.rem(s + ds, S), lax.rem(c + dc, C), t)
-                copy = net.remote(r.sm, r.smx.at[slot], to)
-                go(copy)
-                small.append(copy)
-    reduce4(OUT)
-    reduce4(QKV)
-    for copy in small:
-        copy.wait_recv()
-
-    def add_slot(n, total):
-        return total + r.smx[n]
-
-    r.smo[...] = lax.fori_loop(1, S * C, add_slot, r.smx[0])
-    for name in grads:
-        red[name, 4].wait_recv()
+
+    def spread_small(mine, slots):
+        slots[slot] = mine[...]
+        for ds in range(S):
+            for dc in range(C):
+                if ds or dc:
+                    to = (lax.rem(s + ds, S), lax.rem(c + dc, C), t)
+                    copy = net.remote(mine, slots.at[slot], to)
+                    go(copy)
+                    small.append(copy)
+
+    def small_early():
+        for k in (0, 1, 4, 5, 6, 7):
+            r.sm[k : k + 1, :] = jnp.sum(r.acc[k], axis=0, keepdims=True)
+        spread_small(r.sm, r.smx)
+
+    def small_late():
+        n = D // 4
+        for k in range(2):
+            total = jnp.sum(r.acc[2 + k], axis=0, keepdims=True)
+            for q in range(4):
+                r.smt[4 * k + q : 4 * k + q + 1, :] = total[:, q * n : (q + 1) * n]
+        spread_small(r.smt, r.smtx)
+
+    def finish():
+        for full, home, pieces in (
+            (r.fdn, r.fdn_h, (DN0, DN1)),
+            (r.fup, r.fup_h, (UP0, UP1)),
+            (r.fout, r.fout_h, (OUT0,)),
+            (r.fqkv, r.fqkv_h, (Q0, K0, V0)),
+        ):
+            for p in pieces:
+                red[p, 4].wait_recv()
+            put = net.local(full, home)
+            put.start()
+            puts.append(put)
+        for copy in small:
+            copy.wait_recv()
+        r.smo[...] = lax.fori_loop(1, S * C, lambda n, x: x + r.smx[n], r.smx[0])
+        r.smto[...] = lax.fori_loop(1, S * C, lambda n, x: x + r.smtx[n], r.smtx[0])
+        for put in puts:
+            put.wait()
+        for _, copy in sent:
+            copy.wait_send()
+
+        @pl.when(edge)
+        def _():
+            for copy in hop0.values():
+                copy.wait_send()
+
+        @pl.when(inner)
+        def _():
+            for copy in (*hop1.values(), *hop2.values()):
+                copy.wait_send()
+
+    steps = {
+        LN: first_norm, FW: pass_on, KVP: keys_values, QP: queries, KF: key_forward,
+        AT: attention, P1: attn_part, SS: sum_start, SJ: sum_block, SM: sum_mid, SE: sum_end,
+        MO: middle_of, FF: feed_forward, P3: norm2_part, P2: out_part, MB: middle_back,
+        AB: attention_back, KM: key_mid, KE: key_end, P4: norm1_part, OR: out_rows,
+        TR: token_rows, GD: grad_down, GU: grad_up, GO: grad_out, GQ: grad_proj, R2: reduce2,
+        R3: reduce3, R4: reduce4, SMA: small_early, SMB: small_late, FIN: finish,
+    }
+    for step in ORDER:
+        steps[step[0]](*step[1:])
+
+
+def last_kernel(d, names, *refs):
+    r = types.SimpleNamespace(**dict(zip(names, refs)))
+    pairs = (
+        (r.fdn_i, r.fdn_v, r.fdn_w, r.fdn_o),
+        (r.fup_i, r.fup_v, r.fup_w, r.fup_o),
+        (r.fqkv_i, r.fqkv_v, r.fqkv_w, r.fqkv_o),
+        (r.fout_i, r.fout_v, r.fout_w, r.fout_o),
+        (r.out_i, None, r.out_w, r.out_o),
+        (r.gtok_i, None, r.gtok_w, r.gtok_o),
+    )
+    takes = []
+    for n, (src, low, wide, dst) in enumerate(pairs):
+        takes.append(pltpu.make_async_copy(src, wide if low is None else low, r.sem.at[2 * n]))
+        takes[-1].start()
+    W, D, F = d.local, d.width, d.hidden
+    r.bqv_o[0:1, :] = r.small[0:1, 0:W]
+    r.bqv_o[1:2, :] = r.small[0:1, W : 2 * W]
+    r.bout_o[...] = r.small[1:2, :]
+    r.g2_o[...] = r.small[4:5, :]
+    r.b2_o[...] = r.small[5:6, :]
+    r.bup_o[...] = r.small[6:7, 0:F]
+    r.bdn_o[...] = r.small[7:8, :]
+    n4 = D // 4
+    for q in range(4):
+        w = pl.ds(q * n4, n4)
+        r.g1_o[:, w] = r.late[q : q + 1, :]
+        r.b1_o[:, w] = r.late[4 + q : 5 + q, :]
+    puts = []
+    for n, (src, low, wide, dst) in enumerate(pairs):
+        takes[n].wait()
+        if low is not None:
+            planes = [(low.at[k], wide.at[k]) for k in range(3)] if len(low.shape) == 3 else [(low, wide)]
+            for a, b in planes:
+                step_rows = 64 if a.shape[0] % 64 == 0 else RB
+
+                def step(k, _, a=a, b=b, m=step_rows):
+                    w = span(k, m)
+                    b[w, :] = a[w, :].astype(F32)
+                    return 0
+
+                lax.fori_loop(0, a.shape[0] // step_rows, step, 0)
+        puts.append(pltpu.make_async_copy(wide, dst, r.sem.at[2 * n + 1]))
+        puts[-1].start()
     for put in puts:
         put.wait()
-    for _, copy in sent:
-        copy.wait_send()
-
-    @pl.when(edge)
-    def _():
-        for copy in hop0.values():
-            copy.wait_send()
-
-    @pl.when(inner)
-    def _():
-        for copy in hop1.values():
-            copy.wait_send()
-        for copy in hop2.values():
-            copy.wait_send()
+
+
+def call_last(d, out, gtok, fqkv, fout, fup, fdn, small, late):
+    I, D, W, F = d.images, d.width, d.local, d.hidden
+    arr = jax.ShapeDtypeStruct
+    ins = dict(out_i=out, gtok_i=gtok, fqkv_i=fqkv, fout_i=fout, fup_i=fup, fdn_i=fdn)
+    ins.update(small=small, late=late)
+    outs = dict(out_o=arr(out.shape, F32), gtok_o=arr(gtok.shape, F32))
+    outs.update(fqkv_o=arr(fqkv.shape, F32), fout_o=arr(fout.shape, F32))
+    outs.update(fup_o=arr(fup.shape, F32), fdn_o=arr(fdn.shape, F32))
+    outs.update(bqv_o=arr((2, W), F32), bout_o=arr((1, D), F32), g1_o=arr((1, D), F32))
+    outs.update(b1_o=arr((1, D), F32), g2_o=arr((1, D), F32), b2_o=arr((1, D), F32))
+    outs.update(bup_o=arr((1, F), F32), bdn_o=arr((1, D), F32))
+    vm = lambda a, t: pltpu.VMEM(a.shape, t)
+    scratch = dict(fqkv_v=vm(fqkv, BF), fout_v=vm(fout, BF), fup_v=vm(fup, BF), fdn_v=vm(fdn, BF))
+    scratch.update(fqkv_w=vm(fqkv, F32), fout_w=vm(fout, F32), fup_w=vm(fup, F32))
+    scratch.update(fdn_w=vm(fdn, F32), out_w=vm(out, F32), gtok_w=vm(gtok, F32))
+    scratch.update(sem=pltpu.SemaphoreType.DMA((12,)))
+    vmem = pl.BlockSpec(memory_space=pltpu.VMEM)
+    hbm = pl.BlockSpec(memory_space=pl.ANY)
+    return pl.pallas_call(
+        functools.partial(last_kernel, d, (*ins, *outs, *scratch)),
+        out_shape=tuple(outs.values()),
+        in_specs=[hbm] * 6 + [vmem] * 2,
+        out_specs=(hbm,) * 6 + (vmem,) * 8,
+        scratch_shapes=list(scratch.values()),
+        compiler_params=pltpu.CompilerParams(vmem_limit_bytes=60 * 2**20),
+        name="results",
+    )(*ins.values())
 
 
 def call_kernel(d, ins):
@@ -796,18 +929,19 @@
     outs = dict(
         out_h=arr((I, d.piece, D), F32),
         gtok_h=arr((I, d.piece, D), F32),
-        fqkv=arr((3, d.part, W), BF),
-        fout=arr((W, d.part), BF),
-        fup=arr((d.part, F), BF),
-        fdn=arr((F, d.part), BF),
+        fqkv_h=arr((3, d.part, W), BF),
+        fout_h=arr((W, d.part), BF),
+        fup_h=arr((d.part, F), BF),
+        fdn_h=arr((F, d.part), BF),
         smo=arr((8, D), F32),
+        smto=arr((8, D // 4), F32),
     )
     names = (*ins, *outs, *scratch)
     return pl.pallas_call(
         functools.partial(body_kernel, d, names),
         out_shape=tuple(outs.values()),
-        in_specs=[hbm] * 6 + [vmem] * 9,
-        out_specs=(hbm, hbm, vmem, vmem, vmem, vmem, vmem),
+        in_specs=[hbm] * 15,
+        out_specs=(hbm,) * 6 + (vmem,) * 2,
         scratch_shapes=list(scratch.values()),
         compiler_params=pltpu.CompilerParams(
             collective_id=0, has_side_effects=True, vmem_limit_bytes=67043328
@@ -826,33 +960,23 @@
         wout_h=w_out,
         wup_h=w_up,
         wdn_h=w_down,
-        mask=pad_mask,
-        g1=row(ln1_gain),
-        b1=row(ln1_shift),
-        bqv=b_qv,
-        bout=row(b_out),
-        g2=row(ln2_gain),
-        b2=row(ln2_shift),
-        bup=row(b_up),
-        bdn=row(b_down),
+        mask_h=pad_mask,
+        g1_h=row(ln1_gain),
+        b1_h=row(ln1_shift),
+        bqv_h=b_qv,
+        bout_h=row(b_out),
+        g2_h=row(ln2_gain),
+        b2_h=row(ln2_shift),
+        bup_h=row(b_up),
+        bdn_h=row(b_down),
     )
-    out, gtok, fqkv, fout, fup, fdn, small = call_kernel(d, ins)
-    W = d.local
+    out, gtok, gqkv, gout, gup, gdn, bqv, bout, g1, b1, g2, b2, bup, bdn = call_last(
+        d, *call_kernel(d, ins)
+    )
+    flat = lambda v: v.reshape(-1)
     return (
-        out,
-        gtok,
-        fqkv.astype(F32),
-        small[0, : 2 * W].reshape(2, W),
-        fout.astype(F32),
-        small[1],
-        small[2],
-        small[3],
-        small[4],
-        small[5],
-        fup.astype(F32),
-        small[6, : d.hidden],
-        fdn.astype(F32),
-        small[7],
+        out, gtok, gqkv, bqv, gout, flat(bout), flat(g1), flat(b1), flat(g2), flat(b2), gup,
+        flat(bup), gdn, flat(bdn),
     )
 
 

time: 233 us -> 140 us (0.60)
  Pallas kernels: 219 us -> 139 us
  local copies, waits for them, and re-layouts: 6.57 us -> 0 us
  other arithmetic: 6.53 us -> 0 us
    pallas_call x1, Pallas kernels: 219 us -> 132 us  [call_kernel(): pl.pallas_call(functools.partial(body_kernel, d, names), out_shape=tuple(...]
    pallas_call x0 -> x1, Pallas kernels: none -> 7.29 us  [call_last(): pl.pallas_call(functools.partial(last_kernel, d, (*ins, *outs, *scratch))...]
    convert_element_type x4 -> x0, other arithmetic: 6.53 us -> none  [the longest x1 2.79 us: body(): fup.astype(F32)]
    unnamed x12 -> x0, local copies, waits for them, and re-layouts: 3.47 us -> none
    slice x2 -> x0, local copies, waits for them, and re-layouts: 2.51 us -> none  [the longest x1 1.77 us: body(): small[7]]
where the time goes in v2:
time: 140 us
  Pallas kernels  139 us (99%)
    pallas_call x1, Pallas kernels, call_kernel(): pl.pallas_call(functools.partial(body_kernel, d, names), out_shape=tuple(...  132 us
    pallas_call x1, Pallas kernels, call_last(): pl.pallas_call(functools.partial(last_kernel, d, (*ins, *outs, *scratch))...  7.29 us

profile of v2, /device:TPU:0, one launch (start us, length us, event | category | flops | bytes accessed | tf_op | source)
XLA Modules:
  0.0 139.7 jit_solution(8275650658943006592)
XLA Ops:
  0.7 131.6 %encoder_layer.1 = (f32[3,152,1024]{2,1,0:T(8,128)}, f32[3,152,1024]{2,1,0:T(8,128)}, bf16[3,512,256]{2,1,0:T(8,128)(2,1)}, bf16[256,512]{1,0:T(8,128)(2,1)}, bf...) custom-call(bf16[3,152,1024]{2,1,0:T(8,128)(2,1)} %refs_0_.1, ...), custom_call_target="tpu_custom_call" | custom-call | tf_op jit(solution)/shard_map/encoder_layer/pallas_call | solution.py:940
  132.3 7.3 %results.1 = (f32[3,152,1024]{2,1,0:T(8,128)}, f32[3,152,1024]{2,1,0:T(8,128)}, f32[3,512,256]{2,1,0:T(8,128)}, f32[256,512]{1,0:T(8,128)}, f32[512,1024]{1,0:T(...) custom-call(f32[3,152,1024]{2,1,0:T(8,128)} %get-tuple-element.36.re, ...), custom_call_target="tpu_custom_call" | custom-call | tf_op jit(solution)/shard_map/results/pallas_call | solution.py:912

commit v3 on v2

--- a/solution.py
+++ b/solution.py
@@ -17,35 +17,49 @@
 TILE = 256
 
 
-KV, Q, OUT, UP, DN = range(5)
+Q, KEY, VAL, OUT, UP, DN = range(6)
 Q0, K0, V0, OUT0, UP0, UP1, DN0, DN1 = range(8)
 PIECES = (DN0, DN1, UP0, UP1, OUT0, Q0, K0, V0)
 (
-    LN, FW, KVP, QP, KF, AT, P1, SS, SJ, SM, SE, MO, FF, P3, P2, MB, AB, KM, KE, P4, OR, TR,
+    LN, FW, KP, QP, KF, AT, P1, SS, SJ, SM, SE, MO, FF, P3, P2, MB, AB, KM, KE, P4, OR, TR,
     GD, GU, GO, GQ, R2, R3, R4, SMA, SMB, FIN,
 ) = range(32)
-CUTS = ((0, 80), (80, 72))
+CUTS = ((0, 32), (32, 32), (64, 32), (96, 32), (128, 24))
 ORDER = (
-    (LN, 2), (LN, 0), (LN, 1), (FW, KV), (KVP, 0), (FW, Q), (QP, 1), (QP, 2), (KVP, 1), (KVP, 2),
-    (KF, 0), (QP, 0), (FW, OUT), (AT, 0), (P1, 0), (SS, 1, 0), (KF, 1), (AT, 1), (KF, 2), (P1, 1),
-    (SM, 1, 0, 0), (SS, 1, 1), (AT, 2), (SM, 1, 0, 1), (SE, 1, 0, 0), (SM, 1, 1, 0), (FW, UP),
-    (SE, 1, 0, 1), (P1, 2), (SM, 1, 1, 1), (SS, 1, 2), (FW, DN), (MO, 0), (SE, 1, 1, 0),
-    (SM, 1, 2, 0), (FF, 0), (P3, 0), (SE, 1, 1, 1), (SM, 1, 2, 1), (SS, 3, 0), (MO, 1), (FF, 1),
-    (SE, 1, 2, 0), (P3, 1), (SS, 3, 1), (P2, 0), (SE, 1, 2, 1), (MO, 2), (SM, 3, 0, 0), (FF, 2),
-    (P3, 2), (SM, 3, 0, 1), (SS, 3, 2), (GD,), (SJ, 2, 0, 1), (SE, 3, 0, 0), (P2, 1), (SM, 3, 1, 0),
-    (SJ, 2, 1, 0), (GU,), (SE, 3, 0, 1), (SM, 3, 1, 1), (R2, DN0), (P2, 2), (MB, 0), (SE, 3, 1, 0),
-    (SM, 3, 2, 0), (AB, 0), (SM, 3, 2, 1), (SE, 3, 1, 1), (SJ, 2, 2, 1), (KM, 0), (R3, DN0),
-    (R2, DN1), (SJ, 2, 1, 1), (MB, 1), (SJ, 2, 0, 0), (SM, 2, 0, 1), (SE, 3, 2, 0), (AB, 1),
-    (SE, 3, 2, 1), (R2, UP1), (SM, 2, 1, 0), (KE, 0), (R2, UP0), (P4, 0), (KM, 1), (SE, 2, 0, 1),
-    (SM, 2, 2, 1), (MB, 2), (SS, 4, 0), (R3, DN1), (SM, 2, 1, 1), (SE, 2, 1, 0), (AB, 2),
-    (SE, 2, 2, 1), (SM, 2, 0, 0), (KE, 1), (P4, 1), (SS, 4, 1), (KM, 2), (GO,), (SM, 4, 0, 0),
-    (SE, 2, 1, 1), (GQ, 0), (R3, UP0), (OR, 1), (R4, DN1), (R2, Q0), (SM, 4, 0, 1), (R3, UP1),
-    (SE, 2, 0, 0), (KE, 2), (P4, 2), (SM, 4, 1, 0), (SS, 4, 2), (GQ, 2), (SE, 4, 0, 0), (OR, 0),
-    (R2, OUT0), (GQ, 1), (SJ, 2, 2, 0), (R3, Q0), (SE, 4, 0, 1), (R2, K0), (SM, 4, 1, 1), (R4, UP0),
-    (TR, 0), (SE, 4, 1, 0), (R2, V0), (SM, 4, 2, 0), (SE, 4, 1, 1), (R3, K0), (SM, 4, 2, 1),
-    (R4, Q0), (SMA,), (TR, 1), (R3, OUT0), (SE, 4, 2, 0), (R3, V0), (R4, DN0), (SM, 2, 2, 0),
-    (SE, 4, 2, 1), (SE, 2, 2, 0), (R4, UP1), (R4, OUT0), (TR, 2), (SMB,), (R4, K0), (R4, V0),
-    (OR, 2), (FIN,),
+    (LN, 0), (LN, 2), (FW, KEY), (LN, 1), (KP, 0, 0), (FW, VAL), (KP, 1, 0), (KF, 0, 0), (KP, 0, 2),
+    (KP, 0, 1), (FW, Q), (KP, 1, 2), (KP, 1, 1), (KF, 1, 0), (FW, OUT), (QP, 0), (AT, 0), (P1, 0),
+    (SS, 1, 0), (QP, 1), (KF, 0, 1), (SM, 1, 0, 0), (SM, 1, 0, 1), (KF, 1, 1), (QP, 2), (KF, 1, 2),
+    (SM, 1, 0, 2), (KF, 0, 2), (AT, 1), (SM, 1, 0, 3), (P1, 1), (FW, UP), (SE, 1, 0, 2),
+    (SM, 1, 0, 4), (SS, 1, 1), (SE, 1, 0, 1), (SM, 1, 1, 0), (SE, 1, 0, 0), (AT, 2), (SM, 1, 1, 2),
+    (SE, 1, 0, 3), (SM, 1, 1, 1), (SM, 1, 1, 3), (P1, 2), (SE, 1, 0, 4), (SE, 1, 1, 2), (SS, 1, 2),
+    (SM, 1, 2, 0), (SE, 1, 1, 0), (FW, DN), (MO, 0), (SM, 1, 1, 4), (SM, 1, 2, 1), (SE, 1, 1, 3),
+    (SM, 1, 2, 2), (SE, 1, 1, 1), (FF, 0), (SE, 1, 1, 4), (SM, 1, 2, 4), (SE, 1, 2, 0), (P3, 0),
+    (SS, 3, 0), (MO, 1), (SM, 1, 2, 3), (FF, 1), (SE, 1, 2, 2), (SE, 1, 2, 1), (SE, 1, 2, 4),
+    (P3, 1), (SM, 3, 0, 0), (SE, 1, 2, 3), (SS, 3, 1), (P2, 1), (SM, 3, 0, 1), (P2, 0), (MO, 2),
+    (SJ, 2, 0, 2), (FF, 2), (SM, 3, 0, 2), (SM, 3, 0, 3), (P3, 2), (SE, 3, 0, 1), (SM, 3, 0, 4),
+    (SS, 3, 2), (GU,), (SJ, 2, 1, 0), (SE, 3, 0, 0), (SM, 3, 1, 1), (SM, 3, 1, 2), (SE, 3, 0, 2),
+    (GD,), (SJ, 2, 1, 4), (SM, 3, 1, 0), (R2, UP0), (SJ, 2, 0, 4), (SE, 3, 0, 4), (SJ, 2, 1, 2),
+    (SE, 3, 0, 3), (P2, 2), (SM, 2, 0, 2), (SM, 3, 1, 3), (SM, 3, 1, 4), (MB, 0), (R2, UP1),
+    (SE, 3, 1, 1), (SM, 3, 2, 0), (SE, 3, 1, 2), (AB, 0), (SE, 3, 1, 0), (R2, DN1), (SJ, 2, 2, 0),
+    (SM, 3, 2, 3), (KM, 0), (SE, 3, 1, 3), (SJ, 2, 0, 3), (R3, UP0), (SM, 3, 2, 4), (SE, 3, 1, 4),
+    (SM, 3, 2, 1), (SJ, 2, 1, 3), (SJ, 2, 0, 1), (SJ, 2, 2, 2), (MB, 1), (SM, 3, 2, 2),
+    (SE, 3, 2, 0), (SE, 3, 2, 3), (SM, 2, 1, 0), (SJ, 2, 2, 3), (SM, 2, 1, 4), (AB, 1),
+    (SE, 3, 2, 4), (SM, 2, 0, 4), (KE, 0), (SM, 2, 2, 0), (SE, 3, 2, 1), (R2, DN0), (SE, 3, 2, 2),
+    (SM, 2, 0, 3), (P4, 0), (KM, 1), (SS, 4, 0), (SM, 2, 1, 2), (SE, 2, 1, 4), (SE, 2, 1, 0),
+    (MB, 2), (SE, 2, 0, 2), (SM, 2, 0, 1), (SJ, 2, 1, 1), (R3, DN1), (SM, 2, 1, 3), (AB, 2),
+    (SE, 2, 2, 0), (SM, 2, 2, 2), (SJ, 2, 2, 1), (SE, 2, 0, 3), (KE, 1), (P4, 1), (SE, 2, 0, 4),
+    (SE, 2, 0, 1), (SM, 4, 0, 1), (GO,), (GQ, 0), (SJ, 2, 0, 0), (KM, 2), (SE, 2, 1, 2), (R3, DN0),
+    (SM, 4, 0, 3), (SM, 4, 0, 4), (SS, 4, 1), (SM, 4, 0, 2), (R2, OUT0), (SE, 4, 0, 1),
+    (SM, 2, 1, 1), (SE, 2, 1, 3), (KE, 2), (SE, 2, 2, 2), (SM, 2, 0, 0), (R3, UP1), (SMA,),
+    (SM, 4, 0, 0), (SE, 4, 0, 2), (P4, 2), (SM, 2, 2, 1), (SE, 4, 0, 4), (SE, 2, 0, 0), (SS, 4, 2),
+    (R2, Q0), (SJ, 2, 2, 4), (SM, 4, 1, 1), (SM, 4, 1, 0), (SE, 2, 1, 1), (SM, 4, 1, 3),
+    (SE, 4, 0, 0), (GQ, 1, 2), (SM, 4, 1, 4), (R4, DN1), (R3, OUT0), (SE, 4, 0, 3), (SM, 4, 1, 2),
+    (SE, 4, 1, 1), (SM, 4, 2, 1), (R2, V0), (OR, 1), (OR, 0), (R4, DN0), (SE, 4, 1, 0), (R3, Q0),
+    (SE, 4, 1, 4), (R4, UP0), (SE, 4, 1, 3), (SM, 4, 2, 2), (TR, 0), (SE, 4, 1, 2), (SM, 4, 2, 4),
+    (SM, 4, 2, 0), (SM, 2, 2, 3), (R3, V0), (R2, K0), (SE, 4, 2, 2), (SE, 4, 2, 4), (SM, 4, 2, 3),
+    (SE, 4, 2, 0), (SE, 4, 2, 1), (SM, 2, 2, 4), (R3, K0), (R4, UP1), (SE, 4, 2, 3), (SE, 2, 2, 3),
+    (R4, OUT0), (TR, 1), (R4, Q0), (TR, 2), (R4, V0), (SE, 2, 2, 4), (SMB,), (SE, 2, 2, 1),
+    (R4, K0), (OR, 2), (FIN,),
 )
 
 
@@ -175,36 +189,38 @@
     scratch.update(tot1=full(), tot2=full(), tot3=full(), tot4=full())
     scratch.update(in01=full(), in02=full(), in03=full())
     scratch.update(in11=full(), in12=full(), in13=full())
-    scratch["ssem"] = pltpu.SemaphoreType.DMA((MAX_COPIES * S // 2,))
-    scratch["rsem"] = pltpu.SemaphoreType.DMA((MAX_COPIES * S // 2,))
-    scratch["lsem"] = pltpu.SemaphoreType.DMA((64,))
+    scratch.update(ssem=pltpu.SemaphoreType.DMA((n_sends(d),)))
+    scratch.update(rsem=pltpu.SemaphoreType.DMA((n_recvs(d),)))
+    scratch.update(lsem=pltpu.SemaphoreType.DMA((7 * I + 13,)))
     return scratch
 
 
-MAX_COPIES = 320
+def n_sends(d):
+    return 12 * (d.S - 1) + 8 + 6 + 8 * d.S + 2
+
+
+def n_recvs(d):
+    return 12 * (d.S - 1) + 24 * len(CUTS) + 6 * d.images + 8 * (d.S + 2) + 2
 
 
 class Net:
     def __init__(self, ssem, rsem, lsem):
         self.ssem, self.rsem, self.lsem = ssem, rsem, lsem
-        self.n = self.m = 0
-        self.sent = []
-        self.stored = []
-
-    def remote(self, src, dst, device):
-        i, self.n = self.n, self.n + 1
+        self.sends, self.recvs, self.locals = {}, {}, 0
+
+    def remote(self, src, dst, device, send, recv):
         return pltpu.make_async_remote_copy(
             src_ref=src,
             dst_ref=dst,
-            send_sem=self.ssem.at[i],
-            recv_sem=self.rsem.at[i],
+            send_sem=self.ssem.at[self.sends.setdefault(send, len(self.sends))],
+            recv_sem=self.rsem.at[self.recvs.setdefault(recv, len(self.recvs))],
             device_id=device,
             device_id_type=MESH,
         )
 
     def local(self, src, dst):
-        i, self.m = self.m, self.m + 1
-        return pltpu.make_async_copy(src, dst, self.lsem.at[i])
+        n, self.locals = self.locals, self.locals + 1
+        return pltpu.make_async_copy(src, dst, self.lsem.at[n])
 
 
 def body_kernel(d, names, *refs):
@@ -222,11 +238,19 @@
     edge = lax.rem(t + 1, 4) < 2
     on_mate, on_across = (s, mate, t), (s, across, t)
     net = Net(r.ssem, r.rsem, r.lsem)
-    sent = net.sent
-
-    def go(copy):
+    sent = []
+
+    last = {}
+
+    def go(copy, group=None, whole=None):
         copy.start()
-        sent.append((None, copy))
+        if group is None:
+            sent.append(copy)
+        else:
+            last[group] = whole
+
+    def drain(key, whole):
+        net.remote(whole, whole, on_mate, key, next(iter(net.recvs))).wait_send()
 
     tail = piece // 16 * 16
     for ref in (r.tot1, r.tot2, r.tot3, r.tot4, r.in01, r.in02, r.in03, r.in11, r.in12, r.in13):
@@ -268,8 +292,8 @@
         )
     ]
     rows_s = span(s, part)
-    loads[KV] = net.local(r.wqkv_h.at[pl.ds(1, 2)], r.wqkv.at[pl.ds(1, 2), rows_s])
-    loads[Q] = net.local(r.wqkv_h.at[pl.ds(0, 1)], r.wqkv.at[pl.ds(0, 1), rows_s])
+    for n in (KEY, VAL, Q):
+        loads[n] = net.local(r.wqkv_h.at[n], r.wqkv.at[n, rows_s])
     loads[OUT] = net.local(r.wout_h, r.wout.at[:, rows_s])
     loads[UP] = net.local(r.wup_h, r.wup.at[rows_s])
     loads[DN] = net.local(r.wdn_h, r.wdn.at[:, rows_s])
@@ -288,9 +312,8 @@
 
     def half_of(name, ref, shard, half):
         rows = pl.ds(aligned(shard * part, part), part)
-        if name in (KV, Q):
-            planes = pl.ds(1, 2) if name == KV else pl.ds(0, 1)
-            return ref.at[planes, rows, pl.ds(aligned(half * (W // 2), W // 2), W // 2)]
+        if name in (Q, KEY, VAL):
+            return ref.at[name, rows, span(half, W // 2)]
         if name == OUT:
             return ref.at[pl.ds(aligned(half * (W // 2), W // 2), W // 2), rows]
         if name == UP:
@@ -298,9 +321,8 @@
         return ref.at[pl.ds(aligned(half * (F // 2), F // 2), F // 2), rows]
 
     def own_half(name, ref, half):
-        if name in (KV, Q):
-            planes = pl.ds(1, 2) if name == KV else pl.ds(0, 1)
-            return ref.at[planes, :, pl.ds(aligned(half * (W // 2), W // 2), W // 2)]
+        if name in (Q, KEY, VAL):
+            return ref.at[name, :, span(half, W // 2)]
         if name == OUT:
             return ref.at[pl.ds(aligned(half * (W // 2), W // 2), W // 2), :]
         if name == UP:
@@ -308,7 +330,8 @@
         return ref.at[pl.ds(aligned(half * (F // 2), F // 2), F // 2), :]
 
     weights = {
-        KV: (r.wqkv_h, r.wqkv),
+        KEY: (r.wqkv_h, r.wqkv),
+        VAL: (r.wqkv_h, r.wqkv),
         Q: (r.wqkv_h, r.wqkv),
         OUT: (r.wout_h, r.wout),
         UP: (r.wup_h, r.wup),
@@ -319,13 +342,13 @@
         for ds in range(1, S):
             to = (lax.rem(s + ds, S), c, t)
             copy = net.remote(
-                own_half(name, source, core), half_of(name, full, s, core), to
+                own_half(name, source, core), half_of(name, full, s, core), to, (FW, name, ds), (FW, name, ds)
             )
             go(copy)
             gather[name, ds] = copy
             owner = lax.rem(s + S - ds, S)
             held = half_of(name, full, owner, core)
-            spread[name, ds] = net.remote(held, held, on_mate)
+            spread[name, ds] = net.remote(held, held, on_mate, (FW, name, -ds), (FW, name, -ds))
 
     def pass_on(name):
         for ds in range(1, S):
@@ -384,28 +407,29 @@
     kv_mate, kv_across, kv_far = {}, {}, {}
     row_w = lax.broadcasted_iota(jnp.int32, (R, W), 0)
 
-    def keys_values(i):
-        weight_ready(KV)
-        x = r.first[i]
-        key = dot(x, r.wqkv[1])
-        flags = jnp.broadcast_to(r.maskw[i : i + 1, :], (R, W))
-        r.kv[c, i, 0] = jnp.where(row_w == piece, flags, key).astype(BF)
-        r.kv[c, i, 1] = (dot(x, r.wqkv[2]) + r.bqv[1:2, :]).astype(BF)
-        mine = r.kv.at[c, i]
-        kv_across[i] = net.remote(mine, mine, on_across)
-        kv_mate[i] = net.remote(mine, mine, on_mate)
-        theirs = r.kv.at[across, i]
-        kv_far[i] = net.remote(theirs, theirs, on_mate)
-        go(kv_across[i])
-        go(kv_mate[i])
+    def key_part(n, i):
+        weight_ready(KEY + n)
+        x = dot(r.first[i], r.wqkv[1 + n])
+        if n == 0:
+            flags = jnp.broadcast_to(r.maskw[i : i + 1, :], (R, W))
+            r.kv[c, i, 0] = jnp.where(row_w == piece, flags, x).astype(BF)
+        else:
+            r.kv[c, i, 1] = (x + r.bqv[1:2, :]).astype(BF)
+        mine = r.kv.at[c, i, n]
+        kv_across[n, i] = net.remote(mine, mine, on_across, (KP, 0), (KP, n, i))
+        kv_mate[n, i] = net.remote(mine, mine, on_mate, (KP, 1), (KF, i))
+        theirs = r.kv.at[across, i, n]
+        kv_far[n, i] = net.remote(theirs, theirs, on_mate, (KP, 2), (KF, i))
+        go(kv_across[n, i], (KP, 0), r.kv.at[0])
+        go(kv_mate[n, i], (KP, 1), r.kv.at[0])
 
     def queries(i):
         weight_ready(Q)
         r.q[i] = (dot(r.first[i], r.wqkv[0]) + r.bqv[0:1, :]).astype(BF)
 
-    def key_forward(i):
-        kv_across[i].wait_recv()
-        go(kv_far[i])
+    def key_forward(n, i):
+        kv_across[n, i].wait_recv()
+        go(kv_far[n, i], (KP, 2), r.kv.at[0])
 
     lane_head = lax.broadcasted_iota(jnp.int32, (R, W), 1) // HD
     scale = 1.0 / math.sqrt(HD)
@@ -430,8 +454,9 @@
         return dot_nt(pick, jnp.concatenate(columns, axis=0))[0:1, :]
 
     def attention(i):
-        kv_far[i].wait_recv()
-        kv_mate[i].wait_recv()
+        pair = r.kv.at[pl.ds(0, 2), i]
+        both = net.remote(pair, pair, on_mate, (KP, 1), (KF, i))
+        both.wait_recv()
         k, v = all_keys(i)
         bias = key_bias(i)
         q = r.q[i].astype(F32)
@@ -446,7 +471,7 @@
             r.wts[i, pl.ds(aligned(h * R, R), R), :] = w
             return jnp.where(mine, dot(w, v), total)
 
-        total = lax.fori_loop(0, heads, head, jnp.zeros((R, W), F32))
+        total = lax.fori_loop(0, heads, head, jnp.zeros((R, W), F32), unroll=True)
         r.att[i] = total.astype(BF)
 
     hop0, hop1, hop2 = {}, {}, {}
@@ -458,9 +483,10 @@
         in1 = (r.in11, r.in12, r.in13, r.in11)[k - 1]
         for j, (first, n) in enumerate(CUTS):
             w = pl.ds(first, n)
-            hop0[k, i, j] = net.remote(own.at[i, w], in0.at[i, w], (s, c, tmate))
-            hop1[k, i, j] = net.remote(own.at[i, w], in1.at[i, w], (s, c, tpeer))
-            hop2[k, i, j] = net.remote(tot.at[i, w], tot.at[i, w], (s, c, tmate))
+            a, b = (SM, k, i, j), (SE, k, i, j)
+            hop0[k, i, j] = net.remote(own.at[i, w], in0.at[i, w], (s, c, tmate), (SM, k), a)
+            hop1[k, i, j] = net.remote(own.at[i, w], in1.at[i, w], (s, c, tpeer), (SM, k), b)
+            hop2[k, i, j] = net.remote(tot.at[i, w], tot.at[i, w], (s, c, tmate), (SE, k), a)
         return own, tot, in0, in1
 
     sums = {(k, i): sum_plan(k, i) for k in range(1, 5) for i in range(I)}
@@ -599,9 +625,9 @@
 
     def reduce1(p):
         red[p, 1] = net.remote(
-            grad_half(p, 1 - core), slot_of(p, r.r1q, r.r1o, r.r1u, r.r1d), on_mate
+            grad_half(p, 1 - core), slot_of(p, r.r1q, r.r1o, r.r1u, r.r1d), on_mate, (R3, p), (R2, p)
         )
-        go(red[p, 1])
+        red[p, 1].start()
 
     def reduce2(p):
         r1, r2 = slot_of(p, r.r1q, r.r1o, r.r1u, r.r1d), slot_of(p, r.r2q, r.r2o, r.r2u, r.r2d)
@@ -609,8 +635,10 @@
         add_into(r1, grad_half(p, core), r1)
         for ds in range(1, S):
             to = lax.rem(s + ds, S)
-            red[p, 2, ds] = net.remote(shard_part(p, r1, to), r2.at[ds], (to, c, t))
-            go(red[p, 2, ds])
+            red[p, 2, ds] = net.remote(
+                shard_part(p, r1, to), r2.at[ds], (to, c, t), (R2, p, ds), (R3, p, ds)
+            )
+            red[p, 2, ds].start()
 
     def reduce3(p):
         r1, r2 = slot_of(p, r.r1q, r.r1o, r.r1u, r.r1d), slot_of(p, r.r2q, r.r2o, r.r2u, r.r2d)
@@ -618,8 +646,9 @@
             red[p, 2, ds].wait_recv()
             mine = shard_part(p, r1, s) if ds == 1 else r2.at[0]
             add_into(r2.at[0], mine, r2.at[ds])
+        red[p, 1].wait_send()
         red[p, 3] = net.remote(
-            r2.at[0], slot_of(p, r.r3q, r.r3o, r.r3u, r.r3d), on_across
+            r2.at[0], slot_of(p, r.r3q, r.r3o, r.r3u, r.r3d), on_across, (R3, p), (R4, p)
         )
         go(red[p, 3])
 
@@ -628,7 +657,9 @@
         red[p, 3].wait_recv()
         mine = final_half(p, core)
         add_into(mine, r2.at[0], slot_of(p, r.r3q, r.r3o, r.r3u, r.r3d))
-        red[p, 4] = net.remote(mine, mine, on_mate)
+        for ds in range(1, S):
+            red[p, 2, ds].wait_send()
+        red[p, 4] = net.remote(mine, mine, on_mate, (R2, p, 1), (FIN, p))
         go(red[p, 4])
 
     def flat(ref, w=None):
@@ -655,12 +686,15 @@
         r.gout[...] = dot_tn(flat(r.att), flat(r.mlow)).astype(BF)
         reduce1(OUT0)
 
-    def grad_proj(n):
+    def grad_proj(*planes):
         def tile(w):
-            r.gqkv[n, w, :] = dot_tn(flat(r.first, w), flat(r.pg.at[n])).astype(BF)
+            x = flat(r.first, w)
+            for n in planes:
+                r.gqkv[n, w, :] = dot_tn(x, flat(r.pg.at[n])).astype(BF)
 
         tiles(D, tile)
-        reduce1(Q0 + n)
+        for n in planes:
+            reduce1(Q0 + n)
 
     def middle_back(i):
         sum_got(3, i)
@@ -699,7 +733,7 @@
             r.dss[w, :] = ds
             return jnp.where(mine, dot(ds, k), total)
 
-        dq = lax.fori_loop(0, heads, head, jnp.zeros((R, W), F32))
+        dq = lax.fori_loop(0, heads, head, jnp.zeros((R, W), F32), unroll=True)
         r.acc[0, :, 0:W] += fold8(dq)
         r.pg[0, i] = dq.astype(BF)
         dk = dot_tn(r.dss[...], r.qst[...]).astype(BF)
@@ -713,18 +747,24 @@
     real = pl.ds(0, piece)
 
     def key_send(i):
-        back_far[i] = net.remote(r.dkv.at[far, i, :, real], r.rxa.at[1, i, :, real], on_mate)
-        back_mate[i] = net.remote(r.dkv.at[mate, i, :, real], r.rxa.at[0, i, :, real], on_mate)
-        go(back_far[i])
-        go(back_mate[i])
+        back_far[i] = net.remote(
+            r.dkv.at[far, i, :, real], r.rxa.at[1, i, :, real], on_mate, (KM, 0), (KM, 0, i)
+        )
+        back_mate[i] = net.remote(
+            r.dkv.at[mate, i, :, real], r.rxa.at[0, i, :, real], on_mate, (KM, 1), (KM, 1, i)
+        )
+        go(back_far[i], (KM, 0), r.rxb.at[:, :, real])
+        go(back_mate[i], (KM, 1), r.rxb.at[:, :, real])
 
     def key_mid(i):
         back_far[i].wait_recv()
         for n in range(2):
             both = r.dkv[across, i, n].astype(F32) + r.rxa[1, i, n].astype(F32)
             r.rxa[1, i, n] = both.astype(BF)
-        back_across[i] = net.remote(r.rxa.at[1, i, :, real], r.rxb.at[i, :, real], on_across)
-        go(back_across[i])
+        back_across[i] = net.remote(
+            r.rxa.at[1, i, :, real], r.rxb.at[i, :, real], on_across, (KM, 2), (KM, 2, i)
+        )
+        go(back_across[i], (KM, 2), r.rxb.at[:, :, real])
 
     def key_end(i):
         back_mate[i].wait_recv()
@@ -778,20 +818,21 @@
     slot = s * C + c
     small = []
 
-    def spread_small(mine, slots):
+    def spread_small(mine, slots, key):
         slots[slot] = mine[...]
         for ds in range(S):
             for dc in range(C):
                 if ds or dc:
                     to = (lax.rem(s + ds, S), lax.rem(c + dc, C), t)
-                    copy = net.remote(mine, slots.at[slot], to)
-                    go(copy)
-                    small.append(copy)
+                    copy = net.remote(mine, slots.at[slot], to, key, key)
+                    copy.start()
+        others = slots.at[pl.ds(0, S * C - 1)]
+        small.append(net.remote(others, others, on_mate, key, key))
 
     def small_early():
         for k in (0, 1, 4, 5, 6, 7):
             r.sm[k : k + 1, :] = jnp.sum(r.acc[k], axis=0, keepdims=True)
-        spread_small(r.sm, r.smx)
+        spread_small(r.sm, r.smx, SMA)
 
     def small_late():
         n = D // 4
@@ -799,7 +840,7 @@
             total = jnp.sum(r.acc[2 + k], axis=0, keepdims=True)
             for q in range(4):
                 r.smt[4 * k + q : 4 * k + q + 1, :] = total[:, q * n : (q + 1) * n]
-        spread_small(r.smt, r.smtx)
+        spread_small(r.smt, r.smtx, SMB)
 
     def finish():
         for full, home, pieces in (
@@ -819,21 +860,27 @@
         r.smto[...] = lax.fori_loop(1, S * C, lambda n, x: x + r.smtx[n], r.smtx[0])
         for put in puts:
             put.wait()
-        for _, copy in sent:
+        for copy in (*sent, *small):
             copy.wait_send()
+        for key, whole in last.items():
+            drain(key, whole)
+        owns, tots = (r.own1, r.own2, r.own3, r.own4), (r.tot1, r.tot2, r.tot3, r.tot4)
 
         @pl.when(edge)
         def _():
-            for copy in hop0.values():
-                copy.wait_send()
+            for k in range(4):
+                drain((SM, k + 1), owns[k].at[:, real])
 
         @pl.when(inner)
         def _():
-            for copy in (*hop1.values(), *hop2.values()):
-                copy.wait_send()
+            for k in range(4):
+                drain((SM, k + 1), owns[k].at[:, real])
+                drain((SE, k + 1), tots[k].at[:, real])
+
+        assert len(net.sends) <= n_sends(d) and len(net.recvs) <= n_recvs(d)
 
     steps = {
-        LN: first_norm, FW: pass_on, KVP: keys_values, QP: queries, KF: key_forward,
+        LN: first_norm, FW: pass_on, KP: key_part, QP: queries, KF: key_forward,
         AT: attention, P1: attn_part, SS: sum_start, SJ: sum_block, SM: sum_mid, SE: sum_end,
         MO: middle_of, FF: feed_forward, P3: norm2_part, P2: out_part, MB: middle_back,
         AB: attention_back, KM: key_mid, KE: key_end, P4: norm1_part, OR: out_rows,

time: 140 us -> 135 us (0.964)
  Pallas kernels: 139 us -> 134 us
    pallas_call x1, Pallas kernels: 132 us -> 127 us  [call_kernel(): pl.pallas_call(functools.partial(body_kernel, d, names), out_shape=tuple(...]
where the time goes in v3:
time: 135 us
  Pallas kernels  134 us (99%)
    pallas_call x1, Pallas kernels, call_kernel(): pl.pallas_call(functools.partial(body_kernel, d, names), out_shape=tuple(...  127 us
    pallas_call x1, Pallas kernels, call_last(): pl.pallas_call(functools.partial(last_kernel, d, (*ins, *outs, *scratch))...  7.29 us

profile of v3, /device:TPU:0, one launch (start us, length us, event | category | flops | bytes accessed | tf_op | source)
XLA Modules:
  0.0 134.8 jit_solution(2687373665196682927)
XLA Ops:
  0.7 126.6 %encoder_layer.1 = (f32[3,152,1024]{2,1,0:T(8,128)}, f32[3,152,1024]{2,1,0:T(8,128)}, bf16[3,512,256]{2,1,0:T(8,128)(2,1)}, bf16[256,512]{1,0:T(8,128)(2,1)}, bf...) custom-call(bf16[3,152,1024]{2,1,0:T(8,128)(2,1)} %refs_0_.1, ...), custom_call_target="tpu_custom_call" | custom-call | tf_op jit(solution)/shard_map/encoder_layer/pallas_call | solution.py:987
  127.3 7.3 %results.1 = (f32[3,152,1024]{2,1,0:T(8,128)}, f32[3,152,1024]{2,1,0:T(8,128)}, f32[3,512,256]{2,1,0:T(8,128)}, f32[256,512]{1,0:T(8,128)}, f32[512,1024]{1,0:T(...) custom-call(f32[3,152,1024]{2,1,0:T(8,128)} %get-tuple-element.36.re, ...), custom_call_target="tpu_custom_call" | custom-call | tf_op jit(solution)/shard_map/results/pallas_call | solution.py:959

commit v4 on v3

--- a/solution.py
+++ b/solution.py
@@ -22,44 +22,47 @@
 PIECES = (DN0, DN1, UP0, UP1, OUT0, Q0, K0, V0)
 (
     LN, FW, KP, QP, KF, AT, P1, SS, SJ, SM, SE, MO, FF, P3, P2, MB, AB, KM, KE, P4, OR, TR,
-    GD, GU, GO, GQ, R2, R3, R4, SMA, SMB, FIN,
-) = range(32)
+    GD, GU, GO, GQ, R2, R3, R4, SMA, SMB, FIN, AC,
+) = range(33)
 CUTS = ((0, 32), (32, 32), (64, 32), (96, 32), (128, 24))
 ORDER = (
-    (LN, 0), (LN, 2), (FW, KEY), (LN, 1), (KP, 0, 0), (FW, VAL), (KP, 1, 0), (KF, 0, 0), (KP, 0, 2),
-    (KP, 0, 1), (FW, Q), (KP, 1, 2), (KP, 1, 1), (KF, 1, 0), (FW, OUT), (QP, 0), (AT, 0), (P1, 0),
-    (SS, 1, 0), (QP, 1), (KF, 0, 1), (SM, 1, 0, 0), (SM, 1, 0, 1), (KF, 1, 1), (QP, 2), (KF, 1, 2),
-    (SM, 1, 0, 2), (KF, 0, 2), (AT, 1), (SM, 1, 0, 3), (P1, 1), (FW, UP), (SE, 1, 0, 2),
-    (SM, 1, 0, 4), (SS, 1, 1), (SE, 1, 0, 1), (SM, 1, 1, 0), (SE, 1, 0, 0), (AT, 2), (SM, 1, 1, 2),
-    (SE, 1, 0, 3), (SM, 1, 1, 1), (SM, 1, 1, 3), (P1, 2), (SE, 1, 0, 4), (SE, 1, 1, 2), (SS, 1, 2),
-    (SM, 1, 2, 0), (SE, 1, 1, 0), (FW, DN), (MO, 0), (SM, 1, 1, 4), (SM, 1, 2, 1), (SE, 1, 1, 3),
-    (SM, 1, 2, 2), (SE, 1, 1, 1), (FF, 0), (SE, 1, 1, 4), (SM, 1, 2, 4), (SE, 1, 2, 0), (P3, 0),
-    (SS, 3, 0), (MO, 1), (SM, 1, 2, 3), (FF, 1), (SE, 1, 2, 2), (SE, 1, 2, 1), (SE, 1, 2, 4),
-    (P3, 1), (SM, 3, 0, 0), (SE, 1, 2, 3), (SS, 3, 1), (P2, 1), (SM, 3, 0, 1), (P2, 0), (MO, 2),
-    (SJ, 2, 0, 2), (FF, 2), (SM, 3, 0, 2), (SM, 3, 0, 3), (P3, 2), (SE, 3, 0, 1), (SM, 3, 0, 4),
-    (SS, 3, 2), (GU,), (SJ, 2, 1, 0), (SE, 3, 0, 0), (SM, 3, 1, 1), (SM, 3, 1, 2), (SE, 3, 0, 2),
-    (GD,), (SJ, 2, 1, 4), (SM, 3, 1, 0), (R2, UP0), (SJ, 2, 0, 4), (SE, 3, 0, 4), (SJ, 2, 1, 2),
-    (SE, 3, 0, 3), (P2, 2), (SM, 2, 0, 2), (SM, 3, 1, 3), (SM, 3, 1, 4), (MB, 0), (R2, UP1),
-    (SE, 3, 1, 1), (SM, 3, 2, 0), (SE, 3, 1, 2), (AB, 0), (SE, 3, 1, 0), (R2, DN1), (SJ, 2, 2, 0),
-    (SM, 3, 2, 3), (KM, 0), (SE, 3, 1, 3), (SJ, 2, 0, 3), (R3, UP0), (SM, 3, 2, 4), (SE, 3, 1, 4),
-    (SM, 3, 2, 1), (SJ, 2, 1, 3), (SJ, 2, 0, 1), (SJ, 2, 2, 2), (MB, 1), (SM, 3, 2, 2),
-    (SE, 3, 2, 0), (SE, 3, 2, 3), (SM, 2, 1, 0), (SJ, 2, 2, 3), (SM, 2, 1, 4), (AB, 1),
-    (SE, 3, 2, 4), (SM, 2, 0, 4), (KE, 0), (SM, 2, 2, 0), (SE, 3, 2, 1), (R2, DN0), (SE, 3, 2, 2),
-    (SM, 2, 0, 3), (P4, 0), (KM, 1), (SS, 4, 0), (SM, 2, 1, 2), (SE, 2, 1, 4), (SE, 2, 1, 0),
-    (MB, 2), (SE, 2, 0, 2), (SM, 2, 0, 1), (SJ, 2, 1, 1), (R3, DN1), (SM, 2, 1, 3), (AB, 2),
-    (SE, 2, 2, 0), (SM, 2, 2, 2), (SJ, 2, 2, 1), (SE, 2, 0, 3), (KE, 1), (P4, 1), (SE, 2, 0, 4),
-    (SE, 2, 0, 1), (SM, 4, 0, 1), (GO,), (GQ, 0), (SJ, 2, 0, 0), (KM, 2), (SE, 2, 1, 2), (R3, DN0),
-    (SM, 4, 0, 3), (SM, 4, 0, 4), (SS, 4, 1), (SM, 4, 0, 2), (R2, OUT0), (SE, 4, 0, 1),
-    (SM, 2, 1, 1), (SE, 2, 1, 3), (KE, 2), (SE, 2, 2, 2), (SM, 2, 0, 0), (R3, UP1), (SMA,),
-    (SM, 4, 0, 0), (SE, 4, 0, 2), (P4, 2), (SM, 2, 2, 1), (SE, 4, 0, 4), (SE, 2, 0, 0), (SS, 4, 2),
-    (R2, Q0), (SJ, 2, 2, 4), (SM, 4, 1, 1), (SM, 4, 1, 0), (SE, 2, 1, 1), (SM, 4, 1, 3),
-    (SE, 4, 0, 0), (GQ, 1, 2), (SM, 4, 1, 4), (R4, DN1), (R3, OUT0), (SE, 4, 0, 3), (SM, 4, 1, 2),
-    (SE, 4, 1, 1), (SM, 4, 2, 1), (R2, V0), (OR, 1), (OR, 0), (R4, DN0), (SE, 4, 1, 0), (R3, Q0),
-    (SE, 4, 1, 4), (R4, UP0), (SE, 4, 1, 3), (SM, 4, 2, 2), (TR, 0), (SE, 4, 1, 2), (SM, 4, 2, 4),
-    (SM, 4, 2, 0), (SM, 2, 2, 3), (R3, V0), (R2, K0), (SE, 4, 2, 2), (SE, 4, 2, 4), (SM, 4, 2, 3),
-    (SE, 4, 2, 0), (SE, 4, 2, 1), (SM, 2, 2, 4), (R3, K0), (R4, UP1), (SE, 4, 2, 3), (SE, 2, 2, 3),
-    (R4, OUT0), (TR, 1), (R4, Q0), (TR, 2), (R4, V0), (SE, 2, 2, 4), (SMB,), (SE, 2, 2, 1),
-    (R4, K0), (OR, 2), (FIN,),
+    (FW, KEY), (LN, 0), (KP, 0, 0), (LN, 2), (FW, VAL), (KP, 1, 0), (FW, Q), (LN, 1), (KF, 0, 0),
+    (KF, 1, 0), (KP, 1, 1), (QP, 0), (FW, OUT), (KP, 0, 1), (AT, 0), (P1, 0), (SM, 1, 0, 1),
+    (SM, 1, 0, 0), (SS, 1, 0), (KP, 0, 2), (KF, 1, 1), (SM, 1, 0, 2), (KF, 0, 1), (QP, 1),
+    (KP, 1, 2), (SM, 1, 0, 3), (AT, 1), (SM, 1, 0, 4), (P1, 1), (SS, 1, 1), (SM, 1, 1, 0),
+    (SE, 1, 0, 2), (SE, 1, 0, 1), (SE, 1, 0, 4), (SE, 1, 0, 0), (SM, 1, 1, 2), (KF, 0, 2),
+    (SE, 1, 0, 3), (KF, 1, 2), (QP, 2), (SE, 1, 1, 0), (SM, 1, 1, 1), (SM, 1, 1, 3), (AT, 2),
+    (P1, 2), (SS, 1, 2), (FW, UP), (SM, 1, 1, 4), (SE, 1, 1, 2), (SM, 1, 2, 0), (FW, DN),
+    (SM, 1, 2, 2), (MO, 0), (SE, 1, 1, 3), (SE, 1, 1, 1), (FF, 0, 0), (SE, 1, 1, 4), (SM, 1, 2, 3),
+    (FF, 0, 1), (SE, 1, 2, 0), (P3, 0, 0), (P3, 0, 1), (SM, 1, 2, 1), (SS, 3, 0), (P2, 0, 0),
+    (SE, 1, 2, 2), (SM, 1, 2, 4), (MO, 1), (FF, 1, 0), (FF, 1, 1), (SE, 1, 2, 3), (P3, 1, 1),
+    (P2, 0, 1), (SM, 3, 0, 0), (SE, 1, 2, 4), (SE, 1, 2, 1), (SM, 3, 0, 1), (P3, 1, 0), (SS, 3, 1),
+    (P2, 1, 1), (SJ, 2, 0, 3), (MO, 2), (SM, 3, 0, 2), (SM, 3, 0, 3), (SM, 3, 0, 4), (SE, 3, 0, 0),
+    (FF, 2, 0), (FF, 2, 1), (SM, 3, 1, 0), (P3, 2, 0), (SE, 3, 0, 2), (P3, 2, 1), (SM, 3, 1, 1),
+    (SS, 3, 2), (SE, 3, 0, 1), (GU, 0), (GU, 1), (GD, 1), (SE, 3, 0, 4), (SM, 3, 1, 2), (P2, 1, 0),
+    (SE, 3, 0, 3), (SE, 3, 1, 0), (R2, UP0), (SJ, 2, 1, 4), (SM, 3, 1, 3), (SJ, 2, 0, 1), (MB, 0),
+    (SM, 3, 1, 4), (SJ, 2, 1, 1), (AB, 0), (SE, 3, 1, 2), (SM, 2, 0, 3), (AC, 0), (SE, 3, 1, 3),
+    (SJ, 2, 0, 0), (SM, 3, 2, 0), (P2, 2, 0), (KM, 0), (P2, 2, 1), (SE, 3, 1, 1), (SM, 3, 2, 2),
+    (R2, UP1), (SM, 3, 2, 1), (R2, DN1), (SE, 3, 1, 4), (GD, 0), (SJ, 2, 1, 2), (MB, 1),
+    (SM, 3, 2, 4), (SE, 3, 2, 0), (SJ, 2, 2, 2), (R3, UP0), (SJ, 2, 1, 0), (SM, 3, 2, 3),
+    (SJ, 2, 1, 3), (SE, 3, 2, 2), (AB, 1), (SE, 3, 2, 1), (KE, 0), (SM, 2, 0, 1), (SM, 2, 1, 4),
+    (SM, 2, 1, 1), (SE, 3, 2, 4), (AC, 1), (SM, 2, 0, 0), (SE, 3, 2, 3), (SE, 2, 0, 3), (P4, 0, 0),
+    (SJ, 2, 0, 4), (R2, DN0), (P4, 0, 1), (SM, 2, 1, 2), (SE, 2, 0, 1), (SS, 4, 0), (KM, 1),
+    (MB, 2), (SM, 2, 2, 2), (SE, 2, 1, 4), (AB, 2), (AC, 2), (SM, 2, 1, 0), (SE, 2, 1, 1),
+    (SJ, 2, 0, 2), (SM, 2, 1, 3), (GQ, 0), (SE, 2, 1, 2), (KM, 2), (KE, 1), (SM, 4, 0, 0),
+    (SE, 2, 0, 0), (P4, 1, 1), (SM, 2, 0, 4), (SE, 2, 1, 0), (P4, 1, 0), (SE, 2, 1, 3), (SS, 4, 1),
+    (R3, UP1), (SJ, 2, 2, 4), (GO,), (SM, 4, 0, 1), (SE, 4, 0, 0), (SE, 2, 0, 4), (KE, 2),
+    (SM, 4, 0, 4), (SE, 2, 2, 2), (P4, 2, 1), (SM, 2, 0, 2), (SM, 4, 0, 2), (SM, 4, 0, 3), (OR, 1),
+    (R3, DN0), (R4, UP0), (SE, 4, 0, 1), (GQ, 1, 2), (R3, DN1), (R2, Q0), (SE, 4, 0, 4),
+    (SM, 4, 1, 2), (SM, 4, 1, 1), (SE, 2, 0, 2), (P4, 2, 0), (SM, 4, 1, 0), (R2, V0), (SE, 4, 0, 2),
+    (SM, 4, 1, 3), (SE, 4, 0, 3), (SS, 4, 2), (SM, 2, 2, 4), (SM, 4, 1, 4), (SE, 4, 1, 2),
+    (SE, 4, 1, 1), (SJ, 2, 2, 1), (OR, 0), (SE, 4, 1, 0), (SE, 4, 1, 3), (R2, OUT0), (SM, 4, 2, 2),
+    (R4, UP1), (SM, 4, 2, 1), (R2, K0), (SM, 4, 2, 0), (SJ, 2, 2, 3), (R3, V0), (SE, 2, 2, 4),
+    (SJ, 2, 2, 0), (TR, 0), (R3, Q0), (SE, 4, 1, 4), (SM, 4, 2, 3), (SM, 4, 2, 4), (SE, 4, 2, 2),
+    (SM, 2, 2, 3), (SE, 4, 2, 1), (R4, DN0), (SM, 2, 2, 0), (R3, OUT0), (SE, 4, 2, 0), (R4, V0),
+    (SM, 2, 2, 1), (SE, 4, 2, 3), (R4, DN1), (R3, K0), (TR, 1), (SE, 4, 2, 4), (SE, 2, 2, 3),
+    (SMA,), (R4, Q0), (TR, 2), (SMB,), (R4, OUT0), (SE, 2, 2, 0), (SE, 2, 2, 1), (R4, K0), (OR, 2),
+    (FIN,),
 )
 
 
@@ -200,7 +203,7 @@
 
 
 def n_recvs(d):
-    return 12 * (d.S - 1) + 24 * len(CUTS) + 6 * d.images + 8 * (d.S + 2) + 2
+    return 12 * (d.S - 1) + 18 * len(CUTS) + 6 * d.images + 8 * (d.S + 2) + 2
 
 
 class Net:
@@ -380,12 +383,15 @@
 
         lax.fori_loop(0, 2, step, 0)
 
-    def tiles(n, fn):
+    def tiles(n, fn, h=None, stride=1):
+        count = n // TILE
+        first = 0 if h is None else h * (count // 2 if stride == 1 else 1)
+
         def step(b, _):
-            fn(pl.ds(aligned(b * TILE, TILE), TILE))
+            fn(span(first + b * stride, TILE))
             return 0
 
-        lax.fori_loop(0, n // TILE, step, 0)
+        lax.fori_loop(0, count if h is None else count // 2, step, 0)
 
     r.acc[...] = jnp.zeros_like(r.acc)
     r.sm[...] = jnp.zeros_like(r.sm)
@@ -476,6 +482,9 @@
 
     hop0, hop1, hop2 = {}, {}, {}
 
+    def lanes_of(k):
+        return 1 if k == 4 else k
+
     def sum_plan(k, i):
         own = (r.own1, r.own2, r.own3, r.own4)[k - 1]
         tot = (r.tot1, r.tot2, r.tot3, r.tot4)[k - 1]
@@ -483,7 +492,7 @@
         in1 = (r.in11, r.in12, r.in13, r.in11)[k - 1]
         for j, (first, n) in enumerate(CUTS):
             w = pl.ds(first, n)
-            a, b = (SM, k, i, j), (SE, k, i, j)
+            a, b = (SM, lanes_of(k), i, j), (SE, lanes_of(k), i, j)
             hop0[k, i, j] = net.remote(own.at[i, w], in0.at[i, w], (s, c, tmate), (SM, k), a)
             hop1[k, i, j] = net.remote(own.at[i, w], in1.at[i, w], (s, c, tpeer), (SM, k), b)
             hop2[k, i, j] = net.remote(tot.at[i, w], tot.at[i, w], (s, c, tmate), (SE, k), a)
@@ -555,11 +564,12 @@
 
         blocks(rows)
 
-    def feed_forward(i):
+    def feed_forward(i, h):
         weight_ready(UP)
         weight_ready(DN)
-        loads[FF, i].wait()
-        clear_tail(r.cot, i)
+        if h == 0:
+            loads[FF, i].wait()
+            clear_tail(r.cot, i)
 
         def tile(w):
             u = dot(r.second[i], r.wup[:, w]) + r.bup[:, w]
@@ -570,19 +580,19 @@
             r.actlow[i, :, w] = g.astype(BF)
             r.acc[6, :, w] += fold8(g)
 
-        tiles(F, tile)
-
-    def norm2_part(i):
+        tiles(F, tile, h)
+
+    def norm2_part(i, h):
         def tile(w):
             r.own3[i, :, w] = dot_nt(r.actlow[i], r.wup[w, :]).astype(BF)
 
-        tiles(D, tile)
-
-    def out_part(i):
+        tiles(D, tile, h)
+
+    def out_part(i, h):
         def tile(w):
             r.own2[i, :, w] = dot(r.activ[i], r.wdn[:, w]).astype(BF)
 
-        tiles(D, tile)
+        tiles(D, tile, h)
 
     tall = (Q0, K0, V0, UP0, UP1)
 
@@ -666,21 +676,21 @@
         v = ref[...] if w is None else ref[:, :, w]
         return v.reshape(I * R, v.shape[-1])
 
-    def grad_down():
+    def grad_down(h):
         def tile(w):
             r.gdn[w, :] = dot_tn(flat(r.activ, w), flat(r.cot)).astype(BF)
 
-        tiles(F, tile)
-        reduce1(DN0)
-        reduce1(DN1)
-
-    def grad_up():
+        tiles(F, tile, h, 2)
+        reduce1(DN0 + h)
+
+    def grad_up(h):
         def tile(w):
             r.gup[w, :] = dot_tn(flat(r.second, w), flat(r.actlow)).astype(BF)
 
-        tiles(D, tile)
-        reduce1(UP0)
-        reduce1(UP1)
+        tiles(D, tile, h)
+        if h == 1:
+            reduce1(UP0)
+            reduce1(UP1)
 
     def grad_out():
         r.gout[...] = dot_tn(flat(r.att), flat(r.mlow)).astype(BF)
@@ -736,6 +746,8 @@
         dq = lax.fori_loop(0, heads, head, jnp.zeros((R, W), F32), unroll=True)
         r.acc[0, :, 0:W] += fold8(dq)
         r.pg[0, i] = dq.astype(BF)
+
+    def key_grads(i):
         dk = dot_tn(r.dss[...], r.qst[...]).astype(BF)
         dv = dot_tn(r.wts[i], r.ost[...]).astype(BF)
         for b in range(C):
@@ -776,14 +788,14 @@
             if n == 1:
                 r.acc[0, :, W : 2 * W] += fold8(both)
 
-    def norm1_part(i):
+    def norm1_part(i, h):
         def tile(w):
             total = dot_nt(r.pg[0, i], r.wqkv[0, w, :])
             total = total + dot_nt(r.pg[1, i], r.wqkv[1, w, :])
             total = total + dot_nt(r.pg[2, i], r.wqkv[2, w, :])
             r.own4[i, :, w] = total.astype(BF)
 
-        tiles(D, tile)
+        tiles(D, tile, h)
 
     puts = []
 
@@ -883,7 +895,7 @@
         LN: first_norm, FW: pass_on, KP: key_part, QP: queries, KF: key_forward,
         AT: attention, P1: attn_part, SS: sum_start, SJ: sum_block, SM: sum_mid, SE: sum_end,
         MO: middle_of, FF: feed_forward, P3: norm2_part, P2: out_part, MB: middle_back,
-        AB: attention_back, KM: key_mid, KE: key_end, P4: norm1_part, OR: out_rows,
+        AB: attention_back, AC: key_grads, KM: key_mid, KE: key_end, P4: norm1_part, OR: out_rows,
         TR: token_rows, GD: grad_down, GU: grad_up, GO: grad_out, GQ: grad_proj, R2: reduce2,
         R3: reduce3, R4: reduce4, SMA: small_early, SMB: small_late, FIN: finish,
     }
@@ -894,16 +906,16 @@
 def last_kernel(d, names, *refs):
     r = types.SimpleNamespace(**dict(zip(names, refs)))
     pairs = (
+        (r.out_i, None, r.out_w, r.out_o),
         (r.fdn_i, r.fdn_v, r.fdn_w, r.fdn_o),
+        (r.gtok_i, None, r.gtok_w, r.gtok_o),
         (r.fup_i, r.fup_v, r.fup_w, r.fup_o),
         (r.fqkv_i, r.fqkv_v, r.fqkv_w, r.fqkv_o),
         (r.fout_i, r.fout_v, r.fout_w, r.fout_o),
-        (r.out_i, None, r.out_w, r.out_o),
-        (r.gtok_i, None, r.gtok_w, r.gtok_o),
     )
     takes = []
     for n, (src, low, wide, dst) in enumerate(pairs):
-        takes.append(pltpu.make_async_copy(src, wide if low is None else low, r.sem.at[2 * n]))
+        takes.append(pltpu.make_async_copy(src, wide if low is None else low, r.sem.at[n]))
         takes[-1].start()
     W, D, F = d.local, d.width, d.hidden
     r.bqv_o[0:1, :] = r.small[0:1, 0:W]
@@ -919,23 +931,37 @@
         r.g1_o[:, w] = r.late[q : q + 1, :]
         r.b1_o[:, w] = r.late[4 + q : 5 + q, :]
     puts = []
+
+    def put(src, dst):
+        puts.append(pltpu.make_async_copy(src, dst, r.sem.at[len(pairs) + len(puts)]))
+        puts[-1].start()
+
+    def widen(a, b):
+        m = 64 if a.shape[0] % 64 == 0 else RB
+
+        def step(k, _):
+            w = span(k, m)
+            b[w, :] = a[w, :].astype(F32)
+            return 0
+
+        lax.fori_loop(0, a.shape[0] // m, step, 0)
+
     for n, (src, low, wide, dst) in enumerate(pairs):
         takes[n].wait()
-        if low is not None:
-            planes = [(low.at[k], wide.at[k]) for k in range(3)] if len(low.shape) == 3 else [(low, wide)]
-            for a, b in planes:
-                step_rows = 64 if a.shape[0] % 64 == 0 else RB
-
-                def step(k, _, a=a, b=b, m=step_rows):
-                    w = span(k, m)
-                    b[w, :] = a[w, :].astype(F32)
-                    return 0
-
-                lax.fori_loop(0, a.shape[0] // step_rows, step, 0)
-        puts.append(pltpu.make_async_copy(wide, dst, r.sem.at[2 * n + 1]))
-        puts[-1].start()
-    for put in puts:
-        put.wait()
+        if low is None:
+            put(wide, dst)
+        elif len(low.shape) == 3:
+            for k in range(low.shape[0]):
+                widen(low.at[k], wide.at[k])
+                put(wide.at[k], dst.at[k])
+        else:
+            rows = low.shape[0] // (2 if low.shape[0] % 128 == 0 else 1)
+            for k in range(low.shape[0] // rows):
+                w = pl.ds(k * rows, rows)
+                widen(low.at[w], wide.at[w])
+                put(wide.at[w], dst.at[w])
+    for copy in puts:
+        copy.wait()
 
 
 def call_last(d, out, gtok, fqkv, fout, fup, fdn, small, late):
@@ -953,7 +979,7 @@
     scratch = dict(fqkv_v=vm(fqkv, BF), fout_v=vm(fout, BF), fup_v=vm(fup, BF), fdn_v=vm(fdn, BF))
     scratch.update(fqkv_w=vm(fqkv, F32), fout_w=vm(fout, F32), fup_w=vm(fup, F32))
     scratch.update(fdn_w=vm(fdn, F32), out_w=vm(out, F32), gtok_w=vm(gtok, F32))
-    scratch.update(sem=pltpu.SemaphoreType.DMA((12,)))
+    scratch.update(sem=pltpu.SemaphoreType.DMA((18,)))
     vmem = pl.BlockSpec(memory_space=pltpu.VMEM)
     hbm = pl.BlockSpec(memory_space=pl.ANY)
     return pl.pallas_call(

time: 135 us -> 133 us (0.985)
  Pallas kernels: 134 us -> 132 us
    pallas_call x1, Pallas kernels: 127 us -> 125 us  [call_kernel(): pl.pallas_call(functools.partial(body_kernel, d, names), out_shape=tuple(...]
where the time goes in v4:
time: 133 us
  Pallas kernels  132 us (99%)
    pallas_call x1, Pallas kernels, call_kernel(): pl.pallas_call(functools.partial(body_kernel, d, names), out_shape=tuple(...  125 us
    pallas_call x1, Pallas kernels, call_last(): pl.pallas_call(functools.partial(last_kernel, d, (*ins, *outs, *scratch))...  6.89 us

profile of v4, /device:TPU:0, one launch (start us, length us, event | category | flops | bytes accessed | tf_op | source)
XLA Modules:
  0.0 132.6 jit_solution(2369561056545358493)
XLA Ops:
  0.7 124.9 %encoder_layer.1 = (f32[3,152,1024]{2,1,0:T(8,128)}, f32[3,152,1024]{2,1,0:T(8,128)}, bf16[3,512,256]{2,1,0:T(8,128)(2,1)}, bf16[256,512]{1,0:T(8,128)(2,1)}, bf...) custom-call(bf16[3,152,1024]{2,1,0:T(8,128)(2,1)} %refs_0_.1, ...), custom_call_target="tpu_custom_call" | custom-call | tf_op jit(solution)/shard_map/encoder_layer/pallas_call | solution.py:1013
  125.6 6.9 %results.1 = (f32[3,152,1024]{2,1,0:T(8,128)}, f32[3,152,1024]{2,1,0:T(8,128)}, f32[3,512,256]{2,1,0:T(8,128)}, f32[256,512]{1,0:T(8,128)}, f32[512,1024]{1,0:T(...) custom-call(f32[3,152,1024]{2,1,0:T(8,128)} %get-tuple-element.36.re, ...), custom_call_target="tpu_custom_call" | custom-call | tf_op jit(solution)/shard_map/results/pallas_call | solution.py:985
